TPU v7x, 256 devices: a whole 4x4x8 slice. The times are simulated.
256 devices in a mesh: lon: 16 (over z, x_hi), lat: 4 (over x_lo, core), head: 4 (over y).
Axes of the slice: x: 4 (x_hi: 2, x_lo: 2; x = x_hi * 2 + x_lo), y: 4, z: 8, core: 2. Of those that a mesh axis runs over, the one named last changes fastest.
Arguments:
- features: bfloat16 [8, 24, 192, 384], P(None, 'lat', 'lon'), may hold values from -6 to 6
- attend_weight: bfloat16 [3, 384, 384], P(None, None, 'head'), may hold values from -0.3125 to 0.3125
- output_weight: bfloat16 [384, 384], P('head'), may hold values from -0.3125 to 0.3125
- bias_table: float32 [64, 12, 3312], P(None, 'head'), may hold values from -3 to 304
- bias_type: int32 [4, 4], P(None, 'lat'), may hold values from 0 to 63
- window_shift: int32 [1], replicated, may hold values from 1 to 11
- grad_out: bfloat16 [8, 24, 192, 384], P(None, 'lat', 'lon'), may hold values from -6 to 6
Outputs:
- feature_grad: bfloat16 [8, 24, 192, 384], P(None, 'lat', 'lon', 'head')
- attend_grad: float32 [3, 384, 384], P(None, None, 'head')
- output_grad: float32 [384, 384], P('head')
- bias_grad: float32 [64, 12, 3312], P(None, 'head')
All inputs are finite; a program needn't handle non-finite values.
Results may differ from a plain program's by a relative error of at most 0.01.
Values may be sent and summed in bfloat16 or wider, within the bound.
A program may use at most 128 MiB of HBM per device.

v0:
```python
import functools

import jax
import jax.numpy as jnp
from jax import lax
from jax.experimental import pallas as pl
from jax.experimental.pallas import tpu as pltpu
from jax.sharding import PartitionSpec as P

F32 = jnp.float32
BF16 = jnp.bfloat16
HEADS = 3
WINS = 4
WIDTH = 96
HEAD = 32
SLOTS = 12
GRID = 72
TOKENS = 144
MODEL = 384
SPAN = 23
TABLE = 3312
TABLE_PAD = 3328
GROUP = 138
SCALE = HEAD ** (-0.5)
VMEM = pl.BlockSpec(memory_space=pltpu.VMEM)
SMEM = pl.BlockSpec(memory_space=pltpu.SMEM)
ANY = pl.BlockSpec(memory_space=pl.ANY)


def dot(a, b, da, db):
    return lax.dot_general(a, b, (((da,), (db,)), ((), ())), preferred_element_type=F32)


def three(x):
    hi = x.astype(BF16)
    rest = x - hi.astype(F32)
    mid = rest.astype(BF16)
    return hi, mid, (rest - mid.astype(F32)).astype(BF16)


def fold_map(ci, shift):
    rows = lax.broadcasted_iota(jnp.int32, (288, 256), 0)
    lane = lax.broadcasted_iota(jnp.int32, (1, 256), 1)
    block = lane // SLOTS
    cj = lane - block * SLOTS
    wrap = jnp.where(ci < shift, 12, 0) - jnp.where(cj < shift, 12, 0)
    target = block * SPAN + (11 + ci) - cj + wrap
    target = jnp.where(lane < TOKENS, target, -1)
    return jnp.where(rows == target, 1.0, 0.0).astype(BF16)


def expand_bias(types, shift, table, tabw, spread, maps, bias):
    for h in range(HEADS):
        for w in range(WINS):
            n = h * WINS + w
            tabw[n : n + 1, 0:TABLE] = table[h, pl.ds(types[w], 1), :]
    spread[...] = jnp.zeros_like(spread)
    for zi in range(2):
        for ai in range(6):
            for zj in range(2):
                at = zi * 1656 + zj * 828 + ai * GROUP
                spread[zi * 6 + ai, 0:12, zj * GROUP : (zj + 1) * GROUP] = tabw[0:12, at : at + GROUP]
    parts = three(spread[...].reshape(192, 288))
    for ci in range(SLOTS):
        chosen = fold_map(ci, shift)
        maps[ci] = chosen
        full = dot(parts[0], chosen, 1, 0) + dot(parts[1], chosen, 1, 0) + dot(parts[2], chosen, 1, 0)
        for n in range(12):
            for k in range(2):
                bias[k, pl.ds(n * SLOTS + ci, 12, stride=TOKENS), :] = full[
                    n * 16 : n * 16 + 12, k * 128 : (k + 1) * 128
                ]


def bias_kernel(types_ref, shift_ref, table, maps, bias, tabw, spread):
    expand_bias([types_ref[w, 0] for w in range(WINS)], shift_ref[0], table, tabw, spread, maps, bias)


def gather_rows(own, east, shift, scratch):
    for c in range(SLOTS):
        mine = c >= shift
        for a in range(6):
            rows = jnp.where(mine, own[a, c].astype(F32), east[a, c].astype(F32))
            for k in range(3):
                scratch[k, (a * SLOTS + c) * 8 : (a * SLOTS + c + 1) * 8, :] = rows[:, k * 128 : (k + 1) * 128]


def window_rows(scratch, w):
    halves = []
    for z in range(2):
        lanes = [scratch[k, pl.ds(2 * w + z, GRID, stride=8), :] for k in range(3)]
        halves.append(jnp.concatenate(lanes, axis=1))
    return jnp.concatenate(halves, axis=0).astype(BF16)


def only(x, h):
    return jnp.concatenate([x[k * HEAD : (k + 1) * HEAD] if k == h else jnp.zeros((HEAD, x.shape[1]), x.dtype) for k in range(HEADS)], axis=0)


def attend(shift, x, xe, g, ge, wt, wo, maps, bias, sums, folded, piece, xs, gs, wflip, scores, fold):
    gather_rows(x, xe, shift, xs)
    gather_rows(g, ge, shift, gs)
    wts = wt[...].reshape(3 * WIDTH, MODEL)
    wos = wo[...]
    wflip[...] = wts.astype(F32).T.astype(BF16)
    grads = []
    for w in range(WINS):
        xw = window_rows(xs, w)
        gw = window_rows(gs, w)
        proj = dot(wts, xw, 1, 1).astype(BF16)
        qt, kt, vt = proj[0:96], proj[96:192], proj[192:288]
        q = dot(xw, wts[0:WIDTH], 1, 1).astype(BF16)
        dat = dot(wos, gw, 1, 1).astype(BF16)
        da = dot(gw, wos, 1, 1).astype(BF16)
        att, dq, dk, dv = [], [], [], []
        for h in range(HEADS):
            n = h * WINS + w
            rows = slice(n * TOKENS, (n + 1) * TOKENS)
            own = slice(h * HEAD, (h + 1) * HEAD)
            added = jnp.concatenate([bias[0, rows, :], bias[1, rows, 0:16]], axis=1)
            logits = dot(q, only(kt, h), 1, 0) * SCALE + added
            logits = jnp.exp(logits - jnp.max(logits, axis=1, keepdims=True))
            soft = logits / jnp.sum(logits, axis=1, keepdims=True)
            half = soft.astype(BF16)
            att.append(dot(vt[own], half, 1, 1))
            dv.append(dot(dat[own], half, 1, 0))
            gsoft = dot(da, only(vt, h), 1, 0)
            gsc = soft * (gsoft - jnp.sum(soft * gsoft, axis=1, keepdims=True))
            scores[0, rows, :] = gsc[:, 0:128]
            scores[1, rows, 0:16] = gsc[:, 128:144]
            gh = gsc.astype(BF16)
            dq.append(dot(kt[own], gh, 1, 1) * SCALE)
            dk.append(dot(qt[own], gh, 1, 0) * SCALE)
        dproj = jnp.concatenate(dq + dk + dv, axis=0).astype(BF16)
        attended = jnp.concatenate(att, axis=0).astype(BF16)
        top = dot(dproj, xw, 1, 0)
        low = dot(attended, gw, 1, 0)
        if w == 0:
            sums[0:288, :] = top
            sums[288:384, :] = low
        else:
            sums[0:288, :] += top
            sums[288:384, :] += low
        back = dot(wflip[...], dproj, 1, 0).astype(BF16)
        piece[:, w * TOKENS : (w + 1) * TOKENS] = back
    piece[:, 576:640] = jnp.zeros((MODEL, 64), BF16)
    total = None
    for ci in range(SLOTS):
        part = jnp.concatenate(
            [scores[0, pl.ds(ci, TOKENS, stride=SLOTS), :], scores[1, pl.ds(ci, TOKENS, stride=SLOTS), :][:, 0:16]], axis=1
        )
        hi = part.astype(BF16)
        lo = (part - hi.astype(F32)).astype(BF16)
        chosen = maps[ci][:, 0:TOKENS]
        term = dot(hi, chosen, 1, 1) + dot(lo, chosen, 1, 1)
        total = term if total is None else total + term
    for k in range(3):
        wide = min(128, 288 - k * 128)
        fold[k, :, 0:wide] = total[:, k * 128 : k * 128 + wide]
    folded[...] = jnp.zeros_like(folded)
    for zi in range(2):
        for ai in range(6):
            got = [fold[k, pl.ds(zi * 6 + ai, 12, stride=12), :] for k in range(3)]
            line = jnp.concatenate(got, axis=1)
            for zj in range(2):
                at = zi * 1656 + zj * 828 + ai * GROUP
                folded[0:12, at : at + GROUP] = line[:, zj * GROUP : (zj + 1) * GROUP]


def attend_kernel(shift_ref, x, xe, g, ge, wt, wo, maps, bias, sums, folded, piece, xs, gs, wflip, scores, fold):
    attend(shift_ref[0], x, xe, g, ge, wt, wo, maps, bias, sums, folded, piece, xs, gs, wflip, scores, fold)


def scatter_types(types, rows, out):
    lane = lax.broadcasted_iota(jnp.int32, (64, 16), 1)
    row = lax.broadcasted_iota(jnp.int32, (64, 16), 0)
    wanted = jnp.zeros((64, 16), jnp.int32)
    for n in range(16):
        wanted = jnp.where(lane == n, types[n], wanted)
    pick = jnp.where(row == wanted, 1.0, 0.0).astype(BF16)
    for h in range(HEADS):
        parts = three(rows(h))
        out[h] = (dot(pick, parts[0], 1, 0) + dot(pick, parts[1], 1, 0) + dot(pick, parts[2], 1, 0))[:, 0:TABLE]


def finish_kernel(types_ref, shift_ref, fsum, own, west, bias_out, feat_out, lines):
    def rows(h):
        return jnp.concatenate([fsum[q, h * WINS : (h + 1) * WINS, :] for q in range(4)], axis=0)

    scatter_types([types_ref[n % 4, n // 4] for n in range(16)], rows, bias_out)
    place_features(shift_ref[0], own, west, feat_out, lines)


def place_features(shift, own, west, feat_out, lines):
    lane = lax.broadcasted_iota(jnp.int32, (1, TOKENS), 1)
    mine = (lane - (lane // SLOTS) * SLOTS) >= shift
    for w in range(WINS):
        cols = slice(w * TOKENS, (w + 1) * TOKENS)
        both = jnp.where(mine, own[:, cols].astype(F32), west[:, cols].astype(F32))
        both = jnp.concatenate([both, jnp.zeros((32, TOKENS), F32)], axis=0).T
        for z in range(2):
            lines[pl.ds(2 * w + z, GRID, stride=8), :] = both[z * GRID : (z + 1) * GRID]
    for a in range(6):
        for c in range(SLOTS):
            at = (a * SLOTS + c) * 8
            feat_out[a, c] = lines[at : at + 8, 0:WIDTH].astype(BF16)


def per_device(features, attend_weight, output_weight, bias_table, bias_type, window_shift, grad_out):
    x = features.transpose(1, 2, 0, 3)
    g = grad_out.transpose(1, 2, 0, 3)
    wt = attend_weight.transpose(0, 2, 1)
    table = bias_table.transpose(1, 0, 2)
    count = lax.axis_size("lon")
    west = [(i, (i - 1) % count) for i in range(count)]
    east = [(i, (i + 1) % count) for i in range(count)]
    xe = lax.ppermute(x, "lon", west)
    ge = lax.ppermute(g, "lon", west)
    maps, bias = pl.pallas_call(
        bias_kernel,
        out_shape=(jax.ShapeDtypeStruct((12, 288, 256), BF16), jax.ShapeDtypeStruct((2, 1728, 128), F32)),
        in_specs=[SMEM, SMEM, VMEM],
        out_specs=(VMEM, VMEM),
        scratch_shapes=[pltpu.VMEM((16, TABLE_PAD), F32), pltpu.VMEM((12, 16, 288), F32)],
        compiler_params=pltpu.CompilerParams(vmem_limit_bytes=40 << 20),
        cost_estimate=pl.CostEstimate(flops=10**10, bytes_accessed=10**7, transcendentals=0),
        name="expand_bias",
    )(bias_type, window_shift, table)
    sums, folded, piece = pl.pallas_call(
        attend_kernel,
        out_shape=(
            jax.ShapeDtypeStruct((MODEL, MODEL), F32),
            jax.ShapeDtypeStruct((16, TABLE_PAD), F32),
            jax.ShapeDtypeStruct((MODEL, 640), BF16),
        ),
        in_specs=[SMEM] + [VMEM] * 8,
        out_specs=(VMEM, VMEM, VMEM),
        scratch_shapes=[
            pltpu.VMEM((3, 576, 128), F32),
            pltpu.VMEM((3, 576, 128), F32),
            pltpu.VMEM((MODEL, 288), BF16),
            pltpu.VMEM((2, 1728, 128), F32),
            pltpu.VMEM((3, TOKENS, 128), F32),
        ],
        compiler_params=pltpu.CompilerParams(vmem_limit_bytes=48 << 20),
        name="attend_backward",
    )(window_shift, x, xe, g, ge, wt, output_weight, maps, bias)
    blocks = lax.all_to_all(piece.reshape(4, WIDTH, 640), "head", 0, 0, tiled=True)
    own = jnp.sum(blocks.astype(F32), axis=0).astype(BF16)
    borrowed = lax.ppermute(own, "lon", east)
    sums = lax.psum(sums, ("lon", "lat"))
    folded = lax.psum(folded, "lon")
    folded = lax.all_gather(folded, "lat")
    types = lax.all_gather(bias_type[:, 0], "lat").T
    bias_grad, feat = pl.pallas_call(
        finish_kernel,
        out_shape=(jax.ShapeDtypeStruct((3, 64, TABLE), F32), jax.ShapeDtypeStruct((6, SLOTS, 8, WIDTH), BF16)),
        in_specs=[SMEM, SMEM, VMEM, VMEM, VMEM],
        out_specs=(VMEM, VMEM),
        scratch_shapes=[pltpu.VMEM((576, 128), F32)],
        compiler_params=pltpu.CompilerParams(vmem_limit_bytes=40 << 20),
        name="finish",
    )(types, window_shift, folded, own, borrowed)
    return (
        feat.transpose(2, 0, 1, 3),
        sums[0:288].reshape(3, WIDTH, MODEL).transpose(0, 2, 1),
        sums[288:384],
        bias_grad.transpose(1, 0, 2),
    )


def solution(mesh):
    placed = (
        P(None, "lat", "lon", None),
        P(None, None, "head"),
        P("head", None),
        P(None, "head", None),
        P(None, "lat"),
        P(),
        P(None, "lat", "lon", None),
    )
    return jax.shard_map(
        per_device,
        mesh=mesh,
        in_specs=placed,
        out_specs=(
            P(None, "lat", "lon", "head"),
            P(None, None, "head"),
            P("head", None),
            P(None, "head", None),
        ),
        check_vma=False,
    )
```

profile of v0, /device:TPU:1, one launch (start us, length us, event | category | flops | bytes accessed | tf_op | source)
XLA Modules:
  0.0 413.0 jit_solution(362922780931891197)
XLA Ops:
  7.2 8.9 %collective-permute-start = (bf16[6,12,8,384]{3,2,1,0:T(8,128)(2,1)}, bf16[6,12,8,384]{3,2,1,0:T(8,128)(2,1)S(1)}, u32[]{:S(2)}, u32[]{:S(2)}) collective-permute-start(bf16[6,12,8,384]{3,2,1,0:T(8,128)(2,1)} %bitcast.15), channel_id=1, source_target_pairs={{0,240},{16,0},{32,16},{48,32},{64,48},{80,64},{96,80},{112,96},{1... | collective-permute-start | bytes 1327112 | tf_op jit(solution)/shard_map/ppermute | solution.py:217
  16.1 0.2 collective-permute-start.1
  17.0 0.7 copy.14.types_ref
  17.7 1.7 copy-done.5
  19.5 3.2 expand_bias.1
  22.7 1.2 copy-done
  23.9 1.4 collective-permute-done.xe
  25.3 9.5 %collective-permute-done.1.ge = bf16[6,12,8,384]{3,2,1,0:T(8,128)(2,1)S(1)} collective-permute-done((bf16[6,12,8,384]{3,2,1,0:T(8,128)(2,1)}, bf16[6,12,8,384]{3,2,1,0:T(8,128)(2,1)S(1)}, u32[]{:S(2)}, u32[]{:S(2)}) %collective-permute-start.1) | collective-permute-done | bytes 442400 | tf_op jit(solution)/shard_map/ppermute | solution.py:218
  34.8 14.8 %attend_backward.1 = (f32[384,384]{1,0:T(8,128)}, f32[16,3328]{1,0:T(8,128)}, bf16[384,640]{1,0:T(8,128)(2,1)}) custom-call(s32[1]{0:T(128)S(6)} %copy.18.shift_ref, bf16[6,12,8,384]{3,2,1,0:T(8,128)(2,1)S(1)} %bitcast.16, bf16[6,12,8,384]{3,2,1,0:T(8,128)(2,1)S(1)} %collective-permute-done.xe, bf16[6,12,8,384]{3,2,1,0:T(8,128)(2,1)S(1)} %bitcast.18, ...), custom_call_target="tpu_custom_call" | custom-call | tf_op jit(solution)/shard_map/attend_backward/pallas_call | solution.py:229
  49.6 4.2 %all-to-all-start = ((bf16[4,96,640]{2,1,0:T(8,128)(2,1)}), bf16[4,96,640]{2,1,0:T(8,128)(2,1)S(1)}, u32[]{:S(2)}, u32[]{:S(2)}) async-start(bf16[4,96,640]{2,1,0:T(8,128)(2,1)} %bitcast.8), calls=%async_computation | async-start | bytes 983040 | tf_op jit(solution)/shard_map/all_to_all | solution.py:248
  53.8 0.6 dynamic-slice
  55.1 0.1 bitcast_dynamic-update-slice_fusion
  55.2 4.8 %all-reduce = s32[16]{0:T(128)S(1)} all-reduce(s32[16]{0:T(128)S(1)} %bitcast_dynamic-update-slice_fusion), channel_id=2, replica_groups=mesh['lon'=16,'lat'=4,'head'=4] {'lat'}, use_global_device_ids=true, to_apply=%add | all-reduce | flops 16 | bytes 128
  60.0 0.1 reshape.16
  60.1 0.1 copy.13
  60.2 0.7 all-to-all-done
  60.9 0.1 reduce_sum.12.own
  61.0 0.1 collective-permute-start.2
  61.1 144.6 %all-reduce.4.cloned.1.call-done = f32[1,16,3328]{2,1,0:T(8,128)} async-done(((f32[1,16,3328]{2,1,0:T(8,128)}), f32[1,16,3328]{2,1,0:T(8,128)}) %all-reduce.4.cloned.1.call-update) | async-done | bytes 213008 | tf_op jit(solution)/shard_map/psum | solution.py:252
  205.7 20.1 %all_gather.11.fsum = f32[4,16,3328]{2,1,0:T(8,128)S(1)} all-gather(f32[1,16,3328]{2,1,0:T(8,128)} %all-reduce.4.cloned.1.call-done), channel_id=1, replica_groups=mesh['lon'=16,'lat'=4,'head'=4] {'lat'}, dimensions={0}, use_global_device_ids=true | all-gather | bytes 1064960 | tf_op jit(solution)/shard_map/all_gather | solution.py:253
  225.8 173.8 %all-reduce.6.cloned.1.call-done = f32[384,384]{1,0:T(8,128)} async-done(((f32[384,384]{1,0:T(8,128)}), f32[384,384]{1,0:T(8,128)}) %all-reduce.6.cloned.1.call-update) | async-done | bytes 589840 | tf_op jit(solution)/shard_map/psum | solution.py:251
  399.5 1.8 slice.8
  401.3 1.6 slice.9
  402.9 3.2 finish.1
  (20 shorter events, 0.1 us)
Async XLA Ops:
  7.2 18.1 %collective-permute-start = (bf16[6,12,8,384]{3,2,1,0:T(8,128)(2,1)}, bf16[6,12,8,384]{3,2,1,0:T(8,128)(2,1)S(1)}, u32[]{:S(2)}, u32[]{:S(2)}) collective-permute-start(bf16[6,12,8,384]{3,2,1,0:T(8,128)(2,1)} %bitcast.15), channel_id=1, source_target_pairs={{0,240},{16,0},{32,16},{48,32},{64,48},{80,64},{96,80},{112,96},{1... | collective-permute-start | bytes 1327112 | tf_op jit(solution)/shard_map/ppermute | solution.py:217
  16.1 18.6 %collective-permute-start.1 = (bf16[6,12,8,384]{3,2,1,0:T(8,128)(2,1)}, bf16[6,12,8,384]{3,2,1,0:T(8,128)(2,1)S(1)}, u32[]{:S(2)}, u32[]{:S(2)}) collective-permute-start(bf16[6,12,8,384]{3,2,1,0:T(8,128)(2,1)} %bitcast.17), channel_id=1, source_target_pairs={{0,240},{16,0},{32,16},{48,32},{64,48},{80,64},{96,80},{112,96},{1... | collective-permute-start | bytes 1327112 | tf_op jit(solution)/shard_map/ppermute | solution.py:218
  17.7 1.7 copy-start.5
  19.4 15.3 %copy-start.1 = (bf16[8,6,12,384]{3,0,2,1:T(8,128)(2,1)S(1)}, bf16[8,6,12,384]{3,0,2,1:T(8,128)(2,1)}, u32[]{:S(2)}) copy-start(bf16[8,6,12,384]{3,0,2,1:T(8,128)(2,1)} %param.7) | copy-start | bytes 1327108
  19.4 15.3 %copy-start.2 = (bf16[8,6,12,384]{3,0,2,1:T(8,128)(2,1)S(1)}, bf16[8,6,12,384]{3,0,2,1:T(8,128)(2,1)}, u32[]{:S(2)}) copy-start(bf16[8,6,12,384]{3,0,2,1:T(8,128)(2,1)} %param.13) | copy-start | bytes 1327108
  19.4 15.3 %copy-start.3 = (bf16[3,384,96]{1,2,0:T(8,128)(2,1)S(1)}, bf16[3,384,96]{1,2,0:T(8,128)(2,1)}, u32[]{:S(2)}) copy-start(bf16[3,384,96]{1,2,0:T(8,128)(2,1)} %param.8) | copy-start | bytes 663556
  19.4 15.3 %copy-start.4 = (bf16[96,384]{1,0:T(8,128)(2,1)S(1)}, bf16[96,384]{1,0:T(8,128)(2,1)}, u32[]{:S(2)}) copy-start(bf16[96,384]{1,0:T(8,128)(2,1)} %wo.1) | copy-start | bytes 221188
  22.7 1.2 copy-start
  34.8 19.1 %copy-start.7 = (u32[256]{0:T(256)S(1)}, u32[256]{0:T(256)}, u32[]{:S(2)}) copy-start(u32[256]{0:T(256)} %constant.9) | copy-start | bytes 3076
  34.8 20.4 %copy-start.6 = (s32[4,1]{0,1:T(1,128)S(1)}, s32[4,1]{0,1:T(1,128)}, u32[]{:S(2)}) copy-start(s32[4,1]{0,1:T(1,128)} %param.11) | copy-start | bytes 52
  49.6 11.3 %all-to-all-start = ((bf16[4,96,640]{2,1,0:T(8,128)(2,1)}), bf16[4,96,640]{2,1,0:T(8,128)(2,1)S(1)}, u32[]{:S(2)}, u32[]{:S(2)}) async-start(bf16[4,96,640]{2,1,0:T(8,128)(2,1)} %bitcast.8), calls=%async_computation | async-start | bytes 983040 | tf_op jit(solution)/shard_map/all_to_all | solution.py:248
  53.8 151.9 %all-reduce.4.cloned.1.call-start = ((), (), s32[]{:S(2)}) async-start(), calls=%async_computation.1 | async-start | bytes 425984 | tf_op jit(solution)/shard_map/psum | solution.py:252
  55.1 344.5 %all-reduce.6.cloned.1.call-start = ((), (), s32[]{:S(2)}) async-start(), calls=%async_computation.2 | async-start | bytes 1179648 | tf_op jit(solution)/shard_map/psum | solution.py:251
  61.0 341.9 %collective-permute-start.2 = (bf16[96,640]{1,0:T(8,128)(2,1)S(1)}, bf16[96,640]{1,0:T(8,128)(2,1)S(1)}, u32[]{:S(2)}, u32[]{:S(2)}) collective-permute-start(bf16[96,640]{1,0:T(8,128)(2,1)S(1)} %reduce_sum.12.own), channel_id=1, source_target_pairs={{0,16},{16,32},{32,48},{48,64},{64,80},{80,96},{96,112},{112,128},... | collective-permute-start | bytes 368648 | tf_op jit(solution)/shard_map/ppermute | solution.py:250
Sparse Core Ops, SparseCore 0:
  57.8 147.8 all-reduce.3
  209.1 190.3 all-reduce.5
where the time goes:
time: 414 us; the launch traced here: 413 us
  waiting for transfers between devices  330 us (80%)
  blocking collectives  24.8 us (6%)
  Pallas kernels  21.3 us (5%)
  between operations  15.4 us (4%)
  starting transfers between devices  13.5 us (3%)
  local copies, waits for them, and re-layouts  7.94 us (2%)
    psum x1, waiting for transfers between devices, per_device(): sums = lax.psum(sums, ('lon', 'lat'))  174 us
    psum x1, waiting for transfers between devices, per_device(): folded = lax.psum(folded, 'lon')  145 us
    all_gather x1, blocking collectives, per_device(): folded = lax.all_gather(folded, 'lat')  20.1 us
    pallas_call x1, Pallas kernels, per_device(): pl.pallas_call(attend_kernel, out_shape=(jax.ShapeDtypeStruct((MODEL, MOD...  14.8 us
    ppermute x1, waiting for transfers between devices, per_device(): ge = lax.ppermute(g, 'lon', west)  9.48 us
    ppermute x1, starting transfers between devices, per_device(): xe = lax.ppermute(x, 'lon', west)  8.93 us
  transfers between devices with their start and end apart: 6, of which 5 were waited for; matrix products, arithmetic and copies ran while one was open for 1% of the time, Pallas kernels for 1%

commit v1 on v0

--- a/solution.py
+++ b/solution.py
@@ -97,7 +97,7 @@
     return jnp.concatenate([x[k * HEAD : (k + 1) * HEAD] if k == h else jnp.zeros((HEAD, x.shape[1]), x.dtype) for k in range(HEADS)], axis=0)
 
 
-def attend(shift, x, xe, g, ge, wt, wo, maps, bias, sums, folded, piece, xs, gs, wflip, scores, fold):
+def attend(types, shift, x, xe, g, ge, wt, wo, maps, bias, sums_out, folded_out, piece, xs, gs, wflip, scores, fold, sums, folded):
     gather_rows(x, xe, shift, xs)
     gather_rows(g, ge, shift, gs)
     wts = wt[...].reshape(3 * WIDTH, MODEL)
@@ -142,8 +142,12 @@
             sums[0:288, :] += top
             sums[288:384, :] += low
         back = dot(wflip[...], dproj, 1, 0).astype(BF16)
-        piece[:, w * TOKENS : (w + 1) * TOKENS] = back
-    piece[:, 576:640] = jnp.zeros((MODEL, 64), BF16)
+        for r in range(4):
+            piece[r, :, w * TOKENS : (w + 1) * TOKENS] = back[r * WIDTH : (r + 1) * WIDTH]
+    for r in range(4):
+        piece[r, :, 576:640] = jnp.zeros((WIDTH, 64), BF16)
+    for i in range(8):
+        sums_out[i] = sums[i * 48 : (i + 1) * 48, :].astype(BF16)
     total = None
     for ci in range(SLOTS):
         part = jnp.concatenate(
@@ -165,29 +169,40 @@
             for zj in range(2):
                 at = zi * 1656 + zj * 828 + ai * GROUP
                 folded[0:12, at : at + GROUP] = line[:, zj * GROUP : (zj + 1) * GROUP]
-
-
-def attend_kernel(shift_ref, x, xe, g, ge, wt, wo, maps, bias, sums, folded, piece, xs, gs, wflip, scores, fold):
-    attend(shift_ref[0], x, xe, g, ge, wt, wo, maps, bias, sums, folded, piece, xs, gs, wflip, scores, fold)
-
-
-def scatter_types(types, rows, out):
-    lane = lax.broadcasted_iota(jnp.int32, (64, 16), 1)
-    row = lax.broadcasted_iota(jnp.int32, (64, 16), 0)
-    wanted = jnp.zeros((64, 16), jnp.int32)
-    for n in range(16):
-        wanted = jnp.where(lane == n, types[n], wanted)
-    pick = jnp.where(row == wanted, 1.0, 0.0).astype(BF16)
+    row = lax.broadcasted_iota(jnp.int32, (16, 512), 0)
+    marks = jnp.zeros((16, 512), jnp.int32)
+    for w in range(WINS):
+        marks = jnp.where(row == 12 + w, types[w], marks)
+    marks = marks.astype(F32)
+    for z in range(8):
+        part = folded[:, z * 512 : (z + 1) * 512]
+        folded_out[z] = jnp.where(row < 12, part, marks).astype(BF16)
+
+
+def attend_kernel(types_ref, shift_ref, *refs):
+    attend([types_ref[w, 0] for w in range(WINS)], shift_ref[0], *refs)
+
+
+def scatter_types(lines, out):
+    marks = jnp.concatenate([lines[q][12:16, 0:1] for q in range(4)], axis=0) * 0.0625
+    lane = lax.broadcasted_iota(jnp.int32, (16, 128), 1).astype(F32)
+    pick = jnp.where(lane == marks, 1.0, 0.0).T[0:64].astype(BF16)
     for h in range(HEADS):
-        parts = three(rows(h))
-        out[h] = (dot(pick, parts[0], 1, 0) + dot(pick, parts[1], 1, 0) + dot(pick, parts[2], 1, 0))[:, 0:TABLE]
-
-
-def finish_kernel(types_ref, shift_ref, fsum, own, west, bias_out, feat_out, lines):
-    def rows(h):
-        return jnp.concatenate([fsum[q, h * WINS : (h + 1) * WINS, :] for q in range(4)], axis=0)
-
-    scatter_types([types_ref[n % 4, n // 4] for n in range(16)], rows, bias_out)
+        rows = jnp.concatenate([lines[q][h * WINS : (h + 1) * WINS, 0:TABLE_PAD] for q in range(4)], axis=0)
+        out[h] = dot(pick, rows.astype(BF16), 1, 0)[:, 0:TABLE]
+
+
+def finish_kernel(shift_ref, sums, folded, own, west, attend_out, output_out, bias_out, feat_out, lines):
+    for i in range(8):
+        part = sums[i].astype(F32)
+        if i < 6:
+            attend_out[i // 2, (i % 2) * 48 : (i % 2) * 48 + 48, :] = part
+        else:
+            output_out[(i - 6) * 48 : (i - 5) * 48, :] = part
+    whole = [
+        jnp.concatenate([folded[xh * 4 + q, z] for z in range(7) for xh in range(2)], axis=1).astype(F32) for q in range(4)
+    ]
+    scatter_types(whole, bias_out)
     place_features(shift_ref[0], own, west, feat_out, lines)
 
 
@@ -206,6 +221,183 @@
             feat_out[a, c] = lines[at : at + 8, 0:WIDTH].astype(BF16)
 
 
+ATTEND_SCRATCH = [
+    pltpu.VMEM((3, 576, 128), F32),
+    pltpu.VMEM((3, 576, 128), F32),
+    pltpu.VMEM((MODEL, 288), BF16),
+    pltpu.VMEM((2, 1728, 128), F32),
+    pltpu.VMEM((3, TOKENS, 128), F32),
+    pltpu.VMEM((MODEL, MODEL), F32),
+    pltpu.VMEM((16, 4096), F32),
+]
+
+
+class Links:
+    def __init__(self, send, recv):
+        self.send, self.recv, self.used, self.sent = send, recv, 0, []
+
+    def copy(self, src, dst, to):
+        k = self.used
+        self.used += 1
+        return pltpu.make_async_remote_copy(
+            src_ref=src,
+            dst_ref=dst,
+            send_sem=self.send.at[k],
+            recv_sem=self.recv.at[k],
+            device_id=to,
+            device_id_type=pl.DeviceIdType.MESH,
+        )
+
+    def start(self, src, dst, to):
+        made = self.copy(src, dst, to)
+        made.start()
+        self.sent.append(made)
+        return made
+
+    def finish(self):
+        for made in self.sent:
+            made.wait_send()
+
+
+def place():
+    lon, lat, head = lax.axis_index("lon"), lax.axis_index("lat"), lax.axis_index("head")
+    z, high = lon // 2, lon % 2
+    low, core = lat // 2, lat % 2
+    return lon, lat, head, z, high, high * 2 + low, core
+
+
+def at_grid(z, x, core):
+    return {"lon": z * 2 + x // 2, "lat": (x % 2) * 2 + core}
+
+
+def meet(peers):
+    barrier = pltpu.get_barrier_semaphore()
+    for peer in peers:
+        pl.semaphore_signal(barrier, inc=1, device_id=peer, device_id_type=pl.DeviceIdType.MESH)
+    pl.semaphore_wait(barrier, len(peers))
+
+
+def reduce_body(net, sums, folded, piece, a_out, f_out, own_out, west_out, a1, f1, p1, a2s, a2, f2s, f2, a3, f3):
+    lon, lat, head, z, high, x, core = place()
+    xc = x * 2 + core
+
+    def zs(k):
+        return {"lon": ((z + k) % 8) * 2 + high}
+
+    def xcs(k):
+        other = (xc + k) % 8
+        return at_grid(z, other // 2, other % 2)
+
+    one = []
+    for k in range(1, 8):
+        one.append(net.start(sums.at[(xc + k) % 8], a1.at[k - 1], xcs(k)))
+    two = []
+    for k in range(1, 8):
+        two.append(net.start(folded.at[(z + k) % 8], f1.at[k - 1], zs(k)))
+    pieces = []
+    for k in range(1, 4):
+        pieces.append(net.start(piece.at[(head + k) % 4], p1.at[k - 1], {"head": (head + k) % 4}))
+
+    total = sums[xc].astype(F32)
+    for k in range(7):
+        one[k].wait_recv()
+        total = total + a1[k].astype(F32)
+    for k in range(8):
+        a2s[k, 0:6, :] = total[k * 6 : (k + 1) * 6]
+        a2s[k, 6:8, :] = jnp.zeros((2, MODEL), F32)
+    three_ = []
+    for k in range(1, 8):
+        three_.append(net.start(a2s.at[(z + k) % 8], a2.at[k - 1], zs(k)))
+
+    lines = folded[z].astype(F32)
+    for k in range(7):
+        two[k].wait_recv()
+        lines = lines + f1[k].astype(F32)
+    f2s[0] = lines[:, 0:256].astype(BF16)
+    f2s[1] = lines[:, 256:512].astype(BF16)
+    four = net.start(f2s.at[1 - high], f2, {"lon": z * 2 + 1 - high})
+
+    feat = piece[head].astype(F32)
+    for k in range(3):
+        pieces[k].wait_recv()
+        feat = feat + p1[k].astype(F32)
+    own_out[...] = feat.astype(BF16)
+    back = net.start(own_out, west_out, {"lon": (lon + 1) % 16})
+
+    four.wait_recv()
+    mine = jnp.where(high == 0, lines[:, 0:256], lines[:, 256:512]) + f2[...].astype(F32)
+    f3[z] = mine.astype(BF16)
+    five = []
+    for k in range(1, 8):
+        five.append(net.start(f3.at[z], f3.at[z], zs(k)))
+
+    block = a2s[z]
+    for k in range(7):
+        three_[k].wait_recv()
+        block = block + a2[k]
+    a3[z] = block
+    six = []
+    for k in range(1, 8):
+        six.append(net.start(a3.at[z], a3.at[z], zs(k)))
+
+    for k in range(7):
+        six[k].wait_recv()
+    a_out[xc] = jnp.concatenate([a3[k][0:6] for k in range(8)], axis=0).astype(BF16)
+    partner = at_grid(z, x, 1 - core)
+    arrive = []
+    for k in range(1, 4):
+        arrive.append(net.start(a_out.at[xc], a_out.at[xc], at_grid(z, (x + k) % 4, core)))
+    cross = [net.start(a_out.at[xc], a_out.at[xc], partner)]
+    for k in range(7):
+        five[k].wait_recv()
+    f_out[xc] = f3[...]
+    arrive_f = []
+    for k in range(1, 4):
+        arrive_f.append(net.start(f3, f_out.at[xc], at_grid(z, (x + k) % 4, core)))
+    cross.append(net.start(f3, f_out.at[xc], partner))
+    for k in range(1, 4):
+        there = ((x + 4 - k) % 4) * 2 + core
+        arrive[k - 1].wait_recv()
+        cross.append(net.start(a_out.at[there], a_out.at[there], partner))
+    for k in range(1, 4):
+        there = ((x + 4 - k) % 4) * 2 + core
+        arrive_f[k - 1].wait_recv()
+        cross.append(net.start(f_out.at[there], f_out.at[there], partner))
+    back.wait_recv()
+    for made in cross:
+        made.wait_recv()
+
+
+REDUCE_SCRATCH = [
+    pltpu.VMEM((7, 48, MODEL), BF16),
+    pltpu.VMEM((7, 16, 512), BF16),
+    pltpu.VMEM((3, WIDTH, 640), BF16),
+    pltpu.VMEM((8, 8, MODEL), F32),
+    pltpu.VMEM((7, 8, MODEL), F32),
+    pltpu.VMEM((2, 16, 256), BF16),
+    pltpu.VMEM((16, 256), BF16),
+    pltpu.VMEM((8, 8, MODEL), F32),
+    pltpu.VMEM((8, 16, 256), BF16),
+]
+
+
+def reduce_peers():
+    lon, lat, head, z, high, x, core = place()
+    xc = x * 2 + core
+    peers = [{"lon": ((z + k) % 8) * 2 + high} for k in range(1, 8)]
+    peers += [at_grid(z, ((xc + k) % 8) // 2, (xc + k) % 2) for k in range(1, 8)]
+    peers += [{"head": (head + k) % 4} for k in range(1, 4)]
+    peers += [{"lon": (lon + 1) % 16}, {"lon": (lon + 15) % 16}]
+    return peers
+
+
+def reduce_kernel(sums, folded, piece, a_out, f_out, own_out, west_out, *scratch):
+    meet(reduce_peers())
+    net = Links(*scratch[-2:])
+    reduce_body(net, sums, folded, piece, a_out, f_out, own_out, west_out, *scratch[:-2])
+    net.finish()
+
+
 def per_device(features, attend_weight, output_weight, bias_table, bias_type, window_shift, grad_out):
     x = features.transpose(1, 2, 0, 3)
     g = grad_out.transpose(1, 2, 0, 3)
@@ -213,7 +405,6 @@
     table = bias_table.transpose(1, 0, 2)
     count = lax.axis_size("lon")
     west = [(i, (i - 1) % count) for i in range(count)]
-    east = [(i, (i + 1) % count) for i in range(count)]
     xe = lax.ppermute(x, "lon", west)
     ge = lax.ppermute(g, "lon", west)
     maps, bias = pl.pallas_call(
@@ -229,42 +420,52 @@
     sums, folded, piece = pl.pallas_call(
         attend_kernel,
         out_shape=(
-            jax.ShapeDtypeStruct((MODEL, MODEL), F32),
-            jax.ShapeDtypeStruct((16, TABLE_PAD), F32),
-            jax.ShapeDtypeStruct((MODEL, 640), BF16),
+            jax.ShapeDtypeStruct((8, 48, MODEL), BF16),
+            jax.ShapeDtypeStruct((8, 16, 512), BF16),
+            jax.ShapeDtypeStruct((4, WIDTH, 640), BF16),
         ),
-        in_specs=[SMEM] + [VMEM] * 8,
+        in_specs=[SMEM] * 2 + [VMEM] * 8,
         out_specs=(VMEM, VMEM, VMEM),
-        scratch_shapes=[
-            pltpu.VMEM((3, 576, 128), F32),
-            pltpu.VMEM((3, 576, 128), F32),
-            pltpu.VMEM((MODEL, 288), BF16),
-            pltpu.VMEM((2, 1728, 128), F32),
-            pltpu.VMEM((3, TOKENS, 128), F32),
-        ],
+        scratch_shapes=ATTEND_SCRATCH,
         compiler_params=pltpu.CompilerParams(vmem_limit_bytes=48 << 20),
         name="attend_backward",
-    )(window_shift, x, xe, g, ge, wt, output_weight, maps, bias)
-    blocks = lax.all_to_all(piece.reshape(4, WIDTH, 640), "head", 0, 0, tiled=True)
-    own = jnp.sum(blocks.astype(F32), axis=0).astype(BF16)
-    borrowed = lax.ppermute(own, "lon", east)
-    sums = lax.psum(sums, ("lon", "lat"))
-    folded = lax.psum(folded, "lon")
-    folded = lax.all_gather(folded, "lat")
-    types = lax.all_gather(bias_type[:, 0], "lat").T
-    bias_grad, feat = pl.pallas_call(
+    )(bias_type, window_shift, x, xe, g, ge, wt, output_weight, maps, bias)
+    sums, folded, own, borrowed = pl.pallas_call(
+        reduce_kernel,
+        out_shape=(
+            jax.ShapeDtypeStruct((8, 48, MODEL), BF16),
+            jax.ShapeDtypeStruct((8, 8, 16, 256), BF16),
+            jax.ShapeDtypeStruct((WIDTH, 640), BF16),
+            jax.ShapeDtypeStruct((WIDTH, 640), BF16),
+        ),
+        in_specs=[VMEM] * 3,
+        out_specs=(VMEM,) * 4,
+        scratch_shapes=REDUCE_SCRATCH + [pltpu.SemaphoreType.DMA((64,)), pltpu.SemaphoreType.DMA((64,))],
+        compiler_params=pltpu.CompilerParams(vmem_limit_bytes=40 << 20, collective_id=1, has_side_effects=True),
+        name="reduce_gradients",
+    )(sums, folded, piece)
+    return finish(window_shift, sums, folded, own, borrowed)
+
+
+def finish(window_shift, sums, folded, own, borrowed):
+    attend_grad, output_grad, bias_grad, feat = pl.pallas_call(
         finish_kernel,
-        out_shape=(jax.ShapeDtypeStruct((3, 64, TABLE), F32), jax.ShapeDtypeStruct((6, SLOTS, 8, WIDTH), BF16)),
-        in_specs=[SMEM, SMEM, VMEM, VMEM, VMEM],
-        out_specs=(VMEM, VMEM),
+        out_shape=(
+            jax.ShapeDtypeStruct((3, WIDTH, MODEL), F32),
+            jax.ShapeDtypeStruct((WIDTH, MODEL), F32),
+            jax.ShapeDtypeStruct((3, 64, TABLE), F32),
+            jax.ShapeDtypeStruct((6, SLOTS, 8, WIDTH), BF16),
+        ),
+        in_specs=[SMEM, VMEM, VMEM, VMEM, VMEM],
+        out_specs=(VMEM,) * 4,
         scratch_shapes=[pltpu.VMEM((576, 128), F32)],
         compiler_params=pltpu.CompilerParams(vmem_limit_bytes=40 << 20),
         name="finish",
-    )(types, window_shift, folded, own, borrowed)
+    )(window_shift, sums, folded, own, borrowed)
     return (
         feat.transpose(2, 0, 1, 3),
-        sums[0:288].reshape(3, WIDTH, MODEL).transpose(0, 2, 1),
-        sums[288:384],
+        attend_grad.transpose(0, 2, 1),
+        output_grad,
         bias_grad.transpose(1, 0, 2),
     )
 

time: 414 us -> 75.9 us (0.18)
  waiting for transfers between devices: 330 us -> 10.8 us
  Pallas kernels: 21.3 us -> 50.8 us
  blocking collectives: 24.8 us -> 0 us
  between operations: 15.4 us -> 1.33 us
  starting transfers between devices: 13.5 us -> 9.16 us
  local copies, waits for them, and re-layouts: 7.94 us -> 3.68 us
    psum x2 -> x0, waiting for transfers between devices: 318 us -> none  [the longest x1 174 us: per_device(): sums = lax.psum(sums, ('lon', 'lat'))]
    pallas_call x2 -> x3, Pallas kernels: 18.1 us -> 47.5 us  [the longest x1 31.4 us: per_device(): pl.pallas_call(reduce_kernel, out_shape=(jax.ShapeDtypeStruct((8, 48, MOD...]
    all_gather x1 -> x0, blocking collectives: 20.1 us -> none  [per_device(): folded = lax.all_gather(folded, 'lat')]
    unnamed x1 -> x0, blocking collectives: 4.75 us -> none
    all_to_all x1 -> x0, starting transfers between devices: 4.19 us -> none  [per_device(): lax.all_to_all(piece.reshape(4, WIDTH, 640), 'head', 0, 0, tiled=True)]
  transfers between devices with their start and end apart: 6 -> 2, of which waited for: 5 -> 2; matrix products, arithmetic and copies ran while one was open for 1% -> 1% of each run, Pallas kernels for 1% -> 4%
where the time goes in v1:
time: 75.9 us; the launch traced here: 75.8 us
  Pallas kernels  50.8 us (67%)
  waiting for transfers between devices  10.8 us (14%)
  starting transfers between devices  9.16 us (12%)
  local copies, waits for them, and re-layouts  3.68 us (5%)
  between operations  1.33 us (2%)
    pallas_call x1, Pallas kernels, per_device(): pl.pallas_call(reduce_kernel, out_shape=(jax.ShapeDtypeStruct((8, 48, MOD...  31.4 us
    pallas_call x1, Pallas kernels, per_device(): pl.pallas_call(attend_kernel, out_shape=(jax.ShapeDtypeStruct((8, 48, MOD...  13.9 us
    ppermute x1, waiting for transfers between devices, per_device(): ge = lax.ppermute(g, 'lon', west)  9.48 us
    ppermute x1, starting transfers between devices, per_device(): xe = lax.ppermute(x, 'lon', west)  8.93 us
    unnamed x13, local copies, waits for them, and re-layouts  3.68 us
    pallas_call x1, Pallas kernels, per_device(): pl.pallas_call(bias_kernel, out_shape=(jax.ShapeDtypeStruct((12, 288, 256...  3.24 us
    pallas_call x1, Pallas kernels, finish(): pl.pallas_call(finish_kernel, out_shape=(jax.ShapeDtypeStruct((3, WIDTH,...  2.25 us
  transfers between devices with their start and end apart: 2, of which 2 were waited for; matrix products, arithmetic and copies ran while one was open for 1% of the time, Pallas kernels for 4%

profile of v1, /device:TPU:1, one launch (start us, length us, event | category | flops | bytes accessed | tf_op | source)
XLA Modules:
  0.0 75.8 jit_solution(17386504658390594880)
XLA Ops:
  0.6 8.9 %collective-permute-start = (bf16[6,12,8,384]{3,2,1,0:T(8,128)(2,1)}, bf16[6,12,8,384]{3,2,1,0:T(8,128)(2,1)S(1)}, u32[]{:S(2)}, u32[]{:S(2)}) collective-permute-start(bf16[6,12,8,384]{3,2,1,0:T(8,128)(2,1)} %bitcast.7), channel_id=1, source_target_pairs={{0,240},{16,0},{32,16},{48,32},{64,48},{80,64},{96,80},{112,96},{1... | collective-permute-start | bytes 1327112 | tf_op jit(solution)/shard_map/ppermute | solution.py:408
  9.6 0.2 collective-permute-start.1
  10.4 0.7 copy.12.types_ref
  11.2 0.0 copy-start.5
  11.2 1.7 %copy-done.5 = f32[64,3,3312]{2,0,1:T(8,128)S(1)} copy-done((f32[64,3,3312]{2,0,1:T(8,128)S(1)}, f32[64,3,3312]{2,0,1:T(8,128)}, u32[]{:S(2)}) %copy-start.5) | copy-done | bytes 2543640
  12.9 0.0 copy-start.1
  12.9 0.0 copy-start.2
  12.9 0.0 copy-start.3
  12.9 0.0 copy-start.4
  12.9 3.2 %expand_bias.1 = (bf16[12,288,256]{2,1,0:T(8,128)(2,1)S(1)}, f32[2,1728,128]{2,1,0:T(8,128)S(1)}) custom-call(s32[4,1]{1,0:T(4,128)S(1)} %copy.12.types_ref, s32[1]{0:T(128)S(6)} %copy.13.shift_ref, f32[3,64,3312]{2,1,0:T(8,128)S(1)} %bitcast.12), custom_call_target="tpu_custom_call" | custom-call | flops 10000000000 | bytes 10000000 | tf_op jit(solution)/shard_map/expand_bias/pallas_call | solution.py:410
  16.2 0.0 copy-start
  16.2 1.2 %copy-done = f32[2,1728,128]{2,1,0:T(8,128)} copy-done((f32[2,1728,128]{2,1,0:T(8,128)}, f32[2,1728,128]{2,1,0:T(8,128)S(1)}, u32[]{:S(2)}) %copy-start) | copy-done | bytes 1769496
  17.4 1.4 %collective-permute-done.refs_1_ = bf16[6,12,8,384]{3,2,1,0:T(8,128)(2,1)S(1)} collective-permute-done((bf16[6,12,8,384]{3,2,1,0:T(8,128)(2,1)}, bf16[6,12,8,384]{3,2,1,0:T(8,128)(2,1)S(1)}, u32[]{:S(2)}, u32[]{:S(2)}) %collective-permute-start) | collective-permute-done | bytes 442400 | tf_op jit(solution)/shard_map/ppermute | solution.py:408
  18.7 9.5 %collective-permute-done.1.refs_3_ = bf16[6,12,8,384]{3,2,1,0:T(8,128)(2,1)S(1)} collective-permute-done((bf16[6,12,8,384]{3,2,1,0:T(8,128)(2,1)}, bf16[6,12,8,384]{3,2,1,0:T(8,128)(2,1)S(1)}, u32[]{:S(2)}, u32[]{:S(2)}) %collective-permute-start.1) | collective-permute-done | bytes 442400 | tf_op jit(solution)/shard_map/ppermute | solution.py:409
  28.2 0.0 copy-done.1
  28.2 0.0 copy-done.2
  28.2 0.0 copy-done.3
  28.2 0.0 copy-done.4
  28.2 13.9 %attend_backward.1 = (bf16[8,48,384]{2,1,0:T(8,128)(2,1)S(1)}, bf16[8,16,512]{2,1,0:T(8,128)(2,1)S(1)}, bf16[4,96,640]{2,1,0:T(8,128)(2,1)S(1)}) custom-call(s32[4,1]{1,0:T(4,128)S(1)} %copy.12.types_ref, s32[1]{0:T(128)S(6)} %copy.13.shift_ref, bf16[6,12,8,384]{3,2,1,0:T(8,128)(2,1)S(1)} %bitcast.8, ...), custom_call_target="tpu_custom_call" | custom-call | tf_op jit(solution)/shard_map/attend_backward/pallas_call | solution.py:420
  42.1 31.4 %reduce_gradients.1 = (bf16[8,48,384]{2,1,0:T(8,128)(2,1)S(1)}, bf16[8,8,16,256]{3,2,1,0:T(8,128)(2,1)S(1)}, bf16[96,640]{1,0:T(8,128)(2,1)S(1)}, bf16[96,640]{1,0:T(8,128)(2,1)S(1)}) custom-call(bf16[8,48,384]{2,1,0:T(8,128)(2,1)S(1)} %get-tuple-element.19.sums, bf16[8,16,512]{2,1,0:T(8,128)(2,1)S(1)} %get-tuple-element.20.folded, ...), custom_call_target="tpu_custom_call" | custom-call | tf_op jit(solution)/shard_map/reduce_gradients/pallas_call | solution.py:433
  73.5 2.3 %finish.1 = (f32[3,96,384]{2,1,0:T(8,128)}, f32[96,384]{1,0:T(8,128)}, f32[3,64,3312]{2,1,0:T(8,128)}, bf16[6,12,8,96]{3,2,1,0:T(8,128)(2,1)}) custom-call(s32[1]{0:T(128)S(6)} %copy.13.shift_ref, bf16[8,48,384]{2,1,0:T(8,128)(2,1)S(1)} %get-tuple-element.22.sums, bf16[8,8,16,256]{3,2,1,0:T(8,128)(2,1)S(1)} %get-tuple-element.23.folded, ...), custom_call_target="tpu_custom_call" | custom-call | tf_op jit(solution)/shard_map/finish/pallas_call | solution.py:451
Async XLA Ops:
  0.6 18.1 %collective-permute-start = (bf16[6,12,8,384]{3,2,1,0:T(8,128)(2,1)}, bf16[6,12,8,384]{3,2,1,0:T(8,128)(2,1)S(1)}, u32[]{:S(2)}, u32[]{:S(2)}) collective-permute-start(bf16[6,12,8,384]{3,2,1,0:T(8,128)(2,1)} %bitcast.7), channel_id=1, source_target_pairs={{0,240},{16,0},{32,16},{48,32},{64,48},{80,64},{96,80},{112,96},{1... | collective-permute-start | bytes 1327112 | tf_op jit(solution)/shard_map/ppermute | solution.py:408
  9.6 18.6 %collective-permute-start.1 = (bf16[6,12,8,384]{3,2,1,0:T(8,128)(2,1)}, bf16[6,12,8,384]{3,2,1,0:T(8,128)(2,1)S(1)}, u32[]{:S(2)}, u32[]{:S(2)}) collective-permute-start(bf16[6,12,8,384]{3,2,1,0:T(8,128)(2,1)} %bitcast.9), channel_id=1, source_target_pairs={{0,240},{16,0},{32,16},{48,32},{64,48},{80,64},{96,80},{112,96},{1... | collective-permute-start | bytes 1327112 | tf_op jit(solution)/shard_map/ppermute | solution.py:409
  11.2 1.7 %copy-start.5 = (f32[64,3,3312]{2,0,1:T(8,128)S(1)}, f32[64,3,3312]{2,0,1:T(8,128)}, u32[]{:S(2)}) copy-start(f32[64,3,3312]{2,0,1:T(8,128)} %param.10) | copy-start | bytes 7630852
  12.9 15.3 %copy-start.1 = (bf16[8,6,12,384]{3,0,2,1:T(8,128)(2,1)S(1)}, bf16[8,6,12,384]{3,0,2,1:T(8,128)(2,1)}, u32[]{:S(2)}) copy-start(bf16[8,6,12,384]{3,0,2,1:T(8,128)(2,1)} %param.7) | copy-start | bytes 1327108
  12.9 15.3 %copy-start.2 = (bf16[8,6,12,384]{3,0,2,1:T(8,128)(2,1)S(1)}, bf16[8,6,12,384]{3,0,2,1:T(8,128)(2,1)}, u32[]{:S(2)}) copy-start(bf16[8,6,12,384]{3,0,2,1:T(8,128)(2,1)} %param.13) | copy-start | bytes 1327108
  12.9 15.3 %copy-start.3 = (bf16[3,384,96]{1,2,0:T(8,128)(2,1)S(1)}, bf16[3,384,96]{1,2,0:T(8,128)(2,1)}, u32[]{:S(2)}) copy-start(bf16[3,384,96]{1,2,0:T(8,128)(2,1)} %param.8) | copy-start | bytes 663556
  12.9 15.3 %copy-start.4 = (bf16[96,384]{1,0:T(8,128)(2,1)S(1)}, bf16[96,384]{1,0:T(8,128)(2,1)}, u32[]{:S(2)}) copy-start(bf16[96,384]{1,0:T(8,128)(2,1)} %refs_5_.1) | copy-start | bytes 221188
  16.2 1.2 %copy-start = (f32[2,1728,128]{2,1,0:T(8,128)}, f32[2,1728,128]{2,1,0:T(8,128)S(1)}, u32[]{:S(2)}) copy-start(f32[2,1728,128]{2,1,0:T(8,128)S(1)} %get-tuple-element.18.refs_7_) | copy-start | bytes 5308420

commit v2 on v0

v2 whole, which is shorter than its diff:
```python
import functools

import jax
import jax.numpy as jnp
from jax import lax
from jax.experimental import pallas as pl
from jax.experimental.pallas import tpu as pltpu
from jax.sharding import PartitionSpec as P

F32 = jnp.float32
BF16 = jnp.bfloat16
HEADS = 3
WINS = 4
WIDTH = 96
HEAD = 32
SLOTS = 12
GRID = 72
TOKENS = 144
MODEL = 384
SPAN = 23
TABLE = 3312
TABLE_PAD = 3328
GROUP = 138
SCALE = HEAD ** (-0.5)
VMEM = pl.BlockSpec(memory_space=pltpu.VMEM)
SMEM = pl.BlockSpec(memory_space=pltpu.SMEM)
ANY = pl.BlockSpec(memory_space=pl.ANY)


def dot(a, b, da, db):
    return lax.dot_general(a, b, (((da,), (db,)), ((), ())), preferred_element_type=F32)


def three(x):
    hi = x.astype(BF16)
    rest = x - hi.astype(F32)
    mid = rest.astype(BF16)
    return hi, mid, (rest - mid.astype(F32)).astype(BF16)


def fold_map(ci, shift):
    rows = lax.broadcasted_iota(jnp.int32, (288, 256), 0)
    lane = lax.broadcasted_iota(jnp.int32, (1, 256), 1)
    block = lane // SLOTS
    cj = lane - block * SLOTS
    wrap = jnp.where(ci < shift, 12, 0) - jnp.where(cj < shift, 12, 0)
    target = block * SPAN + (11 + ci) - cj + wrap
    target = jnp.where(lane < TOKENS, target, -1)
    return jnp.where(rows == target, 1.0, 0.0).astype(BF16)


def expand_bias(types, shift, table, tabw, spread, maps, bias):
    for h in range(HEADS):
        for w in range(WINS):
            n = h * WINS + w
            tabw[n : n + 1, 0:TABLE] = table[h, pl.ds(types[w], 1), :]
    spread[...] = jnp.zeros_like(spread)
    for zi in range(2):
        for ai in range(6):
            for zj in range(2):
                at = zi * 1656 + zj * 828 + ai * GROUP
                spread[zi * 6 + ai, 0:12, zj * GROUP : (zj + 1) * GROUP] = tabw[0:12, at : at + GROUP]
    parts = three(spread[...].reshape(192, 288))
    for ci in range(SLOTS):
        chosen = fold_map(ci, shift)
        maps[ci] = chosen
        full = dot(parts[0], chosen, 1, 0) + dot(parts[1], chosen, 1, 0) + dot(parts[2], chosen, 1, 0)
        for n in range(12):
            for k in range(2):
                bias[k, pl.ds(n * SLOTS + ci, 12, stride=TOKENS), :] = full[
                    n * 16 : n * 16 + 12, k * 128 : (k + 1) * 128
                ]


def window_rows(scratch, w):
    halves = []
    for z in range(2):
        lanes = [scratch[k, pl.ds(2 * w + z, GRID, stride=8), :] for k in range(3)]
        halves.append(jnp.concatenate(lanes, axis=1))
    return jnp.concatenate(halves, axis=0).astype(BF16)


def place_rows(own, borrowed, shift, scratch, first, slots):
    for c in slots:
        for a in range(6):
            rows = own[a, c].astype(F32)
            if borrowed is not None:
                keep = c >= shift if first == 0 else c < shift
                rows = jnp.where(keep, rows, borrowed[a, c - first].astype(F32))
            for k in range(3):
                scratch[k, (a * SLOTS + c) * 8 : (a * SLOTS + c + 1) * 8, :] = rows[:, k * 128 : (k + 1) * 128]


def only(x, h):
    return jnp.concatenate([x[k * HEAD : (k + 1) * HEAD] if k == h else jnp.zeros((HEAD, x.shape[1]), x.dtype) for k in range(HEADS)], axis=0)


def forward(xs, wts, bias, qs, proj_out, softs, atts):
    for w in range(WINS):
        xw = window_rows(xs, w)
        proj = dot(wts, xw, 1, 1).astype(BF16)
        proj_out[w] = proj
        q = dot(xw, wts[0:WIDTH], 1, 1).astype(BF16)
        kt, vt = proj[96:192], proj[192:288]
        att = []
        for h in range(HEADS):
            n = h * WINS + w
            rows = slice(n * TOKENS, (n + 1) * TOKENS)
            added = jnp.concatenate([bias[0, rows, :], bias[1, rows, 0:16]], axis=1)
            logits = dot(q, only(kt, h), 1, 0) * SCALE + added
            logits = jnp.exp(logits - jnp.max(logits, axis=1, keepdims=True))
            soft = logits / jnp.sum(logits, axis=1, keepdims=True)
            softs[n] = soft
            att.append(dot(vt[h * HEAD : (h + 1) * HEAD], soft.astype(BF16), 1, 1))
        atts[w] = jnp.concatenate(att, axis=0).astype(BF16)


def backward(xs, gs, wos, proj_in, softs, atts, scores, sums, dprojs):
    for w in range(WINS):
        xw = window_rows(xs, w)
        gw = window_rows(gs, w)
        proj = proj_in[w]
        qt, kt, vt = proj[0:96], proj[96:192], proj[192:288]
        dat = dot(wos, gw, 1, 1).astype(BF16)
        da = dot(gw, wos, 1, 1).astype(BF16)
        dq, dk, dv = [], [], []
        for h in range(HEADS):
            n = h * WINS + w
            rows = slice(n * TOKENS, (n + 1) * TOKENS)
            own = slice(h * HEAD, (h + 1) * HEAD)
            soft = softs[n]
            dv.append(dot(dat[own], soft.astype(BF16), 1, 0))
            gsoft = dot(da, only(vt, h), 1, 0)
            gsc = soft * (gsoft - jnp.sum(soft * gsoft, axis=1, keepdims=True))
            scores[0, rows, :] = gsc[:, 0:128]
            scores[1, rows, 0:16] = gsc[:, 128:144]
            gh = gsc.astype(BF16)
            dq.append(dot(kt[own], gh, 1, 1) * SCALE)
            dk.append(dot(qt[own], gh, 1, 0) * SCALE)
        dproj = jnp.concatenate(dq + dk + dv, axis=0).astype(BF16)
        dprojs[w] = dproj
        top = dot(dproj, xw, 1, 0)
        low = dot(atts[w], gw, 1, 0)
        if w == 0:
            sums[0:288, :] = top
            sums[288:384, :] = low
        else:
            sums[0:288, :] += top
            sums[288:384, :] += low


def fold_scores(types, scores, maps, fold, folded, folded_out):
    total = None
    for ci in range(SLOTS):
        part = jnp.concatenate(
            [scores[0, pl.ds(ci, TOKENS, stride=SLOTS), :], scores[1, pl.ds(ci, TOKENS, stride=SLOTS), :][:, 0:16]], axis=1
        )
        hi = part.astype(BF16)
        lo = (part - hi.astype(F32)).astype(BF16)
        chosen = maps[ci][:, 0:TOKENS]
        term = dot(hi, chosen, 1, 1) + dot(lo, chosen, 1, 1)
        total = term if total is None else total + term
    for k in range(3):
        wide = min(128, 288 - k * 128)
        fold[k, :, 0:wide] = total[:, k * 128 : k * 128 + wide]
    folded[...] = jnp.zeros_like(folded)
    for zi in range(2):
        for ai in range(6):
            got = [fold[k, pl.ds(zi * 6 + ai, 12, stride=12), :] for k in range(3)]
            line = jnp.concatenate(got, axis=1)
            for zj in range(2):
                at = zi * 1656 + zj * 828 + ai * GROUP
                folded[0:12, at : at + GROUP] = line[:, zj * GROUP : (zj + 1) * GROUP]
    row = lax.broadcasted_iota(jnp.int32, (16, 512), 0)
    marks = jnp.zeros((16, 512), jnp.int32)
    for w in range(WINS):
        marks = jnp.where(row == 12 + w, types[w], marks)
    marks = marks.astype(F32)
    for z in range(8):
        part = folded[:, z * 512 : (z + 1) * 512]
        folded_out[z] = jnp.where(row < 12, part, marks).astype(BF16)


def pieces_out(wflip, dprojs, piece):
    for w in range(WINS):
        back = dot(wflip[...], dprojs[w], 1, 0).astype(BF16)
        for r in range(4):
            piece[r, :, w * TOKENS : (w + 1) * TOKENS] = back[r * WIDTH : (r + 1) * WIDTH]
    for r in range(4):
        piece[r, :, 576:640] = jnp.zeros((WIDTH, 64), BF16)


def scatter_types(lines, out):
    marks = jnp.concatenate([lines[q][12:16, 0:1] for q in range(4)], axis=0) * 0.0625
    lane = lax.broadcasted_iota(jnp.int32, (16, 128), 1).astype(F32)
    pick = jnp.where(lane == marks, 1.0, 0.0).T[0:64].astype(BF16)
    for h in range(HEADS):
        rows = jnp.concatenate([lines[q][h * WINS : (h + 1) * WINS, 0:TABLE_PAD] for q in range(4)], axis=0)
        out[h] = dot(pick, rows.astype(BF16), 1, 0)[:, 0:TABLE]


def finish_kernel(shift_ref, sums, folded, own, west, attend_out, output_out, bias_out, feat_out, lines):
    for i in range(8):
        part = sums[i].astype(F32)
        if i < 6:
            attend_out[i // 2, (i % 2) * 48 : (i % 2) * 48 + 48, :] = part
        else:
            output_out[(i - 6) * 48 : (i - 5) * 48, :] = part
    whole = [
        jnp.concatenate([folded[xh * 4 + q, z] for z in range(7) for xh in range(2)], axis=1).astype(F32) for q in range(4)
    ]
    scatter_types(whole, bias_out)
    place_features(shift_ref[0], own, west, feat_out, lines)


def place_features(shift, own, west, feat_out, lines):
    lane = lax.broadcasted_iota(jnp.int32, (1, TOKENS), 1)
    slot = lane - (lane // SLOTS) * SLOTS
    mine = jnp.where(shift <= 6, slot - shift, shift - 1 - slot) >= 0
    for w in range(WINS):
        cols = slice(w * TOKENS, (w + 1) * TOKENS)
        both = jnp.where(mine, own[:, cols].astype(F32), west[:, cols].astype(F32))
        both = jnp.concatenate([both, jnp.zeros((32, TOKENS), F32)], axis=0).T
        for z in range(2):
            lines[pl.ds(2 * w + z, GRID, stride=8), :] = both[z * GRID : (z + 1) * GRID]
    for a in range(6):
        for c in range(SLOTS):
            at = (a * SLOTS + c) * 8
            feat_out[a, c] = lines[at : at + 8, 0:WIDTH].astype(BF16)


class Links:
    def __init__(self, send, recv):
        self.send, self.recv, self.used, self.sent = send, recv, 0, []

    def copy(self, src, dst, to):
        k = self.used
        self.used += 1
        return pltpu.make_async_remote_copy(
            src_ref=src,
            dst_ref=dst,
            send_sem=self.send.at[k],
            recv_sem=self.recv.at[k],
            device_id=to,
            device_id_type=pl.DeviceIdType.MESH,
        )

    def start(self, src, dst, to):
        made = self.copy(src, dst, to)
        made.start()
        self.sent.append(made)
        return made

    def finish(self):
        for made in self.sent:
            made.wait_send()


def place():
    lon, lat, head = lax.axis_index("lon"), lax.axis_index("lat"), lax.axis_index("head")
    z, high = lon // 2, lon % 2
    low, core = lat // 2, lat % 2
    return lon, lat, head, z, high, high * 2 + low, core


def at_grid(z, x, core):
    return {"lon": z * 2 + x // 2, "lat": (x % 2) * 2 + core}


def meet(peers):
    barrier = pltpu.get_barrier_semaphore()
    for peer in peers:
        pl.semaphore_signal(barrier, inc=1, device_id=peer, device_id_type=pl.DeviceIdType.MESH)
    pl.semaphore_wait(barrier, len(peers))


def reduce_peers():
    lon, lat, head, z, high, x, core = place()
    xc = x * 2 + core
    peers = [{"lon": ((z + k) % 8) * 2 + high} for k in range(1, 8)]
    peers += [at_grid(z, ((xc + k) % 8) // 2, (xc + k) % 2) for k in range(1, 8)]
    peers += [{"head": (head + k) % 4} for k in range(1, 4)]
    peers += [{"lon": (lon + 1) % 16}, {"lon": (lon + 15) % 16}]
    return peers


NAMES = dict(
    xv=pltpu.VMEM((6, SLOTS, 8, MODEL), BF16),
    gv=pltpu.VMEM((6, SLOTS, 8, MODEL), BF16),
    xe=pltpu.VMEM((6, 6, 8, MODEL), BF16),
    ge=pltpu.VMEM((6, 6, 8, MODEL), BF16),
    tabv=pltpu.VMEM((3, 64, TABLE), F32),
    wtv=pltpu.VMEM((3, WIDTH, MODEL), BF16),
    wov=pltpu.VMEM((WIDTH, MODEL), BF16),
    tabw=pltpu.VMEM((16, TABLE_PAD), F32),
    spread=pltpu.VMEM((12, 16, 288), F32),
    maps=pltpu.VMEM((12, 288, 256), BF16),
    bias=pltpu.VMEM((2, 1728, 128), F32),
    xs=pltpu.VMEM((3, 576, 128), F32),
    gs=pltpu.VMEM((3, 576, 128), F32),
    wflip=pltpu.VMEM((MODEL, 288), BF16),
    projs=pltpu.VMEM((WINS, 288, TOKENS), BF16),
    softs=pltpu.VMEM((12, TOKENS, TOKENS), F32),
    atts=pltpu.VMEM((WINS, WIDTH, TOKENS), BF16),
    scores=pltpu.VMEM((2, 1728, 128), F32),
    dprojs=pltpu.VMEM((WINS, 288, TOKENS), BF16),
    fold=pltpu.VMEM((3, TOKENS, 128), F32),
    sums=pltpu.VMEM((MODEL, MODEL), F32),
    folded=pltpu.VMEM((16, 4096), F32),
    a0=pltpu.VMEM((8, 48, MODEL), BF16),
    f0=pltpu.VMEM((8, 16, 512), BF16),
    p0=pltpu.VMEM((4, WIDTH, 640), BF16),
    a1=pltpu.VMEM((7, 48, MODEL), BF16),
    f1=pltpu.VMEM((7, 16, 512), BF16),
    p1=pltpu.VMEM((3, WIDTH, 640), BF16),
    a2s=pltpu.VMEM((8, 8, MODEL), F32),
    a2=pltpu.VMEM((7, 8, MODEL), F32),
    f2s=pltpu.VMEM((2, 16, 256), BF16),
    f2=pltpu.VMEM((16, 256), BF16),
    a3=pltpu.VMEM((8, 8, MODEL), F32),
    f3=pltpu.VMEM((8, 16, 256), BF16),
    send=pltpu.SemaphoreType.DMA((72,)),
    recv=pltpu.SemaphoreType.DMA((72,)),
    load=pltpu.SemaphoreType.DMA((8,)),
)


def main_kernel(first, types_ref, shift_ref, x, g, table, wt, wo, a_out, f_out, own_out, west_out, *scratch):
    v = dict(zip(NAMES, scratch, strict=True))
    lon, lat, head, z, high, xpos, core = place()
    xc = xpos * 2 + core
    step = 1 if first == 0 else 15
    net = Links(v["send"], v["recv"])
    loads = []
    for src, dst in ((x, "xv"), (g, "gv"), (table, "tabv"), (wt, "wtv"), (wo, "wov")):
        made = pltpu.make_async_copy(src, v[dst], v["load"].at[len(loads)])
        made.start()
        loads.append(made)
    types = [types_ref[w, 0] for w in range(WINS)]
    shift = shift_ref[0]
    loads[0].wait()
    loads[1].wait()
    meet(reduce_peers())

    rows, cols = pl.ds((head // 2) * 3, 3), (head % 2) * 3
    giver = {"lon": (lon + 16 - step) % 16}
    halo = []
    for own, far in ((v["xv"], v["xe"]), (v["gv"], v["ge"])):
        part = own.at[rows, pl.ds(first + cols, 3)]
        halo.append(net.start(part, far.at[rows, pl.ds(cols, 3)], giver))
    loads[2].wait()
    expand_bias(types, shift, v["tabv"], v["tabw"], v["spread"], v["maps"], v["bias"])
    spread_out = []
    for k, far in ((0, v["xe"]), (1, v["ge"])):
        halo[k].wait_recv()
        part = far.at[rows, pl.ds(cols, 3)]
        spread_out.append([net.start(part, part, {"head": (head + j) % 4}) for j in range(1, 4)])
    mixed = [c for c in range(first, first + 6)]
    still = [c for c in range(SLOTS) if c not in mixed]
    place_rows(v["xv"], None, shift, v["xs"], first, still)
    place_rows(v["gv"], None, shift, v["gs"], first, still)
    loads[3].wait()
    loads[4].wait()
    wts = v["wtv"][...].reshape(3 * WIDTH, MODEL)
    wos = v["wov"][...]
    v["wflip"][...] = wts.astype(F32).T.astype(BF16)

    for made in spread_out[0]:
        made.wait_recv()
    place_rows(v["xv"], v["xe"], shift, v["xs"], first, mixed)
    forward(v["xs"], wts, v["bias"], None, v["projs"], v["softs"], v["atts"])
    for made in spread_out[1]:
        made.wait_recv()
    place_rows(v["gv"], v["ge"], shift, v["gs"], first, mixed)
    backward(v["xs"], v["gs"], wos, v["projs"], v["softs"], v["atts"], v["scores"], v["sums"], v["dprojs"])

    def zs(k):
        return {"lon": ((z + k) % 8) * 2 + high}

    def xcs(k):
        other = (xc + k) % 8
        return at_grid(z, other // 2, other % 2)

    a0, f0, p0 = v["a0"], v["f0"], v["p0"]
    a1, f1, p1 = v["a1"], v["f1"], v["p1"]
    a2s, a2, f2s, f2, a3, f3 = (v[n] for n in ("a2s", "a2", "f2s", "f2", "a3", "f3"))
    for i in range(8):
        a0[i] = v["sums"][i * 48 : (i + 1) * 48, :].astype(BF16)
    one = [net.start(a0.at[(xc + k) % 8], a1.at[k - 1], xcs(k)) for k in range(1, 8)]
    fold_scores(types, v["scores"], v["maps"], v["fold"], v["folded"], f0)
    two = [net.start(f0.at[(z + k) % 8], f1.at[k - 1], zs(k)) for k in range(1, 8)]
    pieces_out(v["wflip"], v["dprojs"], p0)
    pieces = [net.start(p0.at[(head + k) % 4], p1.at[k - 1], {"head": (head + k) % 4}) for k in range(1, 4)]

    total = a0[xc].astype(F32)
    for k in range(7):
        one[k].wait_recv()
        total = total + a1[k].astype(F32)
    for k in range(8):
        a2s[k, 0:6, :] = total[k * 6 : (k + 1) * 6]
        a2s[k, 6:8, :] = jnp.zeros((2, MODEL), F32)
    three_ = [net.start(a2s.at[(z + k) % 8], a2.at[k - 1], zs(k)) for k in range(1, 8)]

    lines = f0[z].astype(F32)
    for k in range(7):
        two[k].wait_recv()
        lines = lines + f1[k].astype(F32)
    f2s[0] = lines[:, 0:256].astype(BF16)
    f2s[1] = lines[:, 256:512].astype(BF16)
    four = net.start(f2s.at[1 - high], f2, {"lon": z * 2 + 1 - high})

    feat = p0[head].astype(F32)
    for k in range(3):
        pieces[k].wait_recv()
        feat = feat + p1[k].astype(F32)
    own_out[...] = feat.astype(BF16)
    back = net.start(own_out, west_out, {"lon": (lon + step) % 16})

    four.wait_recv()
    mine = jnp.where(high == 0, lines[:, 0:256], lines[:, 256:512]) + f2[...].astype(F32)
    f3[z] = mine.astype(BF16)
    five = [net.start(f3.at[z], f3.at[z], zs(k)) for k in range(1, 8)]

    block = a2s[z]
    for k in range(7):
        three_[k].wait_recv()
        block = block + a2[k]
    a3[z] = block
    six = [net.start(a3.at[z], a3.at[z], zs(k)) for k in range(1, 8)]

    partner = at_grid(z, xpos, 1 - core)
    for k in range(7):
        five[k].wait_recv()
    arrive_f = [net.start(f3, f_out.at[xc], at_grid(z, (xpos + k) % 4, core)) for k in range(1, 4)]
    cross = [net.start(f3, f_out.at[xc], partner)]
    f_out[xc] = f3[...]
    for k in range(7):
        six[k].wait_recv()
    a_out[xc] = jnp.concatenate([a3[k][0:6] for k in range(8)], axis=0).astype(BF16)
    arrive = [net.start(a_out.at[xc], a_out.at[xc], at_grid(z, (xpos + k) % 4, core)) for k in range(1, 4)]
    cross.append(net.start(a_out.at[xc], a_out.at[xc], partner))
    for arrived, out in ((arrive_f, f_out), (arrive, a_out)):
        for k in range(1, 4):
            there = ((xpos + 4 - k) % 4) * 2 + core
            arrived[k - 1].wait_recv()
            cross.append(net.start(out.at[there], out.at[there], partner))
    back.wait_recv()
    for made in cross:
        made.wait_recv()
    net.finish()


def per_device(features, attend_weight, output_weight, bias_table, bias_type, window_shift, grad_out):
    x = features.transpose(1, 2, 0, 3)
    g = grad_out.transpose(1, 2, 0, 3)
    wt = attend_weight.transpose(0, 2, 1)
    table = bias_table.transpose(1, 0, 2)

    def run(first):
        return pl.pallas_call(
            functools.partial(main_kernel, first),
            out_shape=(
                jax.ShapeDtypeStruct((8, 48, MODEL), BF16),
                jax.ShapeDtypeStruct((8, 8, 16, 256), BF16),
                jax.ShapeDtypeStruct((WIDTH, 640), BF16),
                jax.ShapeDtypeStruct((WIDTH, 640), BF16),
            ),
            in_specs=[SMEM] * 2 + [ANY] * 5,
            out_specs=(VMEM,) * 4,
            scratch_shapes=list(NAMES.values()),
            compiler_params=pltpu.CompilerParams(
                vmem_limit_bytes=56 << 20, collective_id=1 if first == 0 else 2, has_side_effects=True
            ),
            name="block_east" if first == 0 else "block_west",
        )

    args = (bias_type, window_shift, x, g, table, wt, output_weight)
    sums, folded, own, borrowed = lax.cond(window_shift[0] <= 6, run(0), run(6), *args)
    return finish(window_shift, sums, folded, own, borrowed)


def finish(window_shift, sums, folded, own, borrowed):
    attend_grad, output_grad, bias_grad, feat = pl.pallas_call(
        finish_kernel,
        out_shape=(
            jax.ShapeDtypeStruct((3, WIDTH, MODEL), F32),
            jax.ShapeDtypeStruct((WIDTH, MODEL), F32),
            jax.ShapeDtypeStruct((3, 64, TABLE), F32),
            jax.ShapeDtypeStruct((6, SLOTS, 8, WIDTH), BF16),
        ),
        in_specs=[SMEM, VMEM, VMEM, VMEM, VMEM],
        out_specs=(VMEM,) * 4,
        scratch_shapes=[pltpu.VMEM((576, 128), F32)],
        compiler_params=pltpu.CompilerParams(vmem_limit_bytes=40 << 20),
        name="finish",
    )(window_shift, sums, folded, own, borrowed)
    return (
        feat.transpose(2, 0, 1, 3),
        attend_grad.transpose(0, 2, 1),
        output_grad,
        bias_grad.transpose(1, 0, 2),
    )


def solution(mesh):
    placed = (
        P(None, "lat", "lon", None),
        P(None, None, "head"),
        P("head", None),
        P(None, "head", None),
        P(None, "lat"),
        P(),
        P(None, "lat", "lon", None),
    )
    return jax.shard_map(
        per_device,
        mesh=mesh,
        in_specs=placed,
        out_specs=(
            P(None, "lat", "lon", "head"),
            P(None, None, "head"),
            P("head", None),
            P(None, "head", None),
        ),
        check_vma=False,
    )
```

time: 414 us -> 61.5 us (0.15)
  waiting for transfers between devices: 330 us -> 0 us
  Pallas kernels: 21.3 us -> 58.5 us
  blocking collectives: 24.8 us -> 0 us
  between operations: 15.4 us -> 1.29 us
  starting transfers between devices: 13.5 us -> 0 us
  local copies, waits for them, and re-layouts: 7.94 us -> 1.31 us
    psum x2 -> x0, waiting for transfers between devices: 318 us -> none  [the longest x1 174 us: per_device(): sums = lax.psum(sums, ('lon', 'lat'))]
    pallas_call x3 -> x2, Pallas kernels: 21.3 us -> 58.5 us  [the longest x1 56.3 us: per_device(): lax.cond(window_shift[0] <= 6, run(0), run(6), *args)]
    all_gather x1 -> x0, blocking collectives: 20.1 us -> none  [per_device(): folded = lax.all_gather(folded, 'lat')]
    ppermute x3 -> x0, waiting for transfers between devices: 10.8 us -> none  [the longest x1 9.48 us: per_device(): ge = lax.ppermute(g, 'lon', west)]
    ppermute x3 -> x0, starting transfers between devices: 9.24 us -> none  [the longest x1 8.93 us: per_device(): xe = lax.ppermute(x, 'lon', west)]
    unnamed x1 -> x0, blocking collectives: 4.75 us -> none
    unnamed x20 -> x0, local copies, waits for them, and re-layouts: 4.38 us -> none
    all_to_all x1 -> x0, starting transfers between devices: 4.19 us -> none  [per_device(): lax.all_to_all(piece.reshape(4, WIDTH, 640), 'head', 0, 0, tiled=True)]
  transfers between devices with their start and end apart: 6 -> 0, of which waited for: 5 -> 0; matrix products, arithmetic and copies ran while one was open for 1% -> 0% of each run, Pallas kernels for 1% -> 0%
where the time goes in v2:
time: 61.5 us; the launch traced here: 61.4 us
  Pallas kernels  58.5 us (95%)
  local copies, waits for them, and re-layouts  1.31 us (2%)
  between operations  1.29 us (2%)
    pallas_call x1, Pallas kernels, per_device(): lax.cond(window_shift[0] <= 6, run(0), run(6), *args)  56.3 us
    pallas_call x1, Pallas kernels, finish(): pl.pallas_call(finish_kernel, out_shape=(jax.ShapeDtypeStruct((3, WIDTH,...  2.25 us
    another operation x1, local copies, waits for them, and re-layouts  1.31 us

profile of v2, /device:TPU:1, one launch (start us, length us, event | category | flops | bytes accessed | tf_op | source)
XLA Modules:
  0.0 61.4 jit_solution(3935699489122473491)
XLA Ops:
  1.3 57.8 %conditional.1 = ((bf16[8,48,384]{2,1,0:T(8,128)(2,1)S(1)}, bf16[8,8,16,256]{3,2,1,0:T(8,128)(2,1)S(1)}, bf16[96,640]{1,0:T(8,128)(2,1)S(1)}, bf16[96,640]{1,0:T(8,128)(2,1)S(1)})) conditional(s32[]{:T(128)} %bitcast, (s32[4,1]{0,1:T(1,128)}, s32[1]{0:T(128)}, bf16[6,12,8,384]{3,2,1,0:T(8,128)(2,1)}, bf16[6,12,8,384]{3,2,1,0:T(8,128)(2,1)}, ...), branch_computations={%region_0.0_spmd, %region_1.0_spmd} | conditional | bytes 40 | solution.py:478
  1.3 1.3 %copy.11.types_ref = s32[4,1]{1,0:T(4,128)} copy(s32[4,1]{0,1:T(1,128)} %get-tuple-element.62) | data formatting | bytes 32 | tf_op jit(solution)/shard_map
  2.6 56.3 %block_west.1 = (bf16[8,48,384]{2,1,0:T(8,128)(2,1)S(1)}, bf16[8,8,16,256]{3,2,1,0:T(8,128)(2,1)S(1)}, bf16[96,640]{1,0:T(8,128)(2,1)S(1)}, bf16[96,640]{1,0:T(8,128)(2,1)S(1)}) custom-call(s32[4,1]{1,0:T(4,128)} %copy.11.types_ref, s32[1]{0:T(128)} %get-tuple-element.29.shift_ref, bf16[6,12,8,384]{3,2,1,0:T(8,128)(2,1)} %get-tuple-element.30.x, ...), custom_call_target="tpu_custom_call" | custom-call | tf_op jit(solution)/shard_map/cond/branch_0_fun/block_west/pallas_call | solution.py:478
  59.1 2.3 %finish.1 = (f32[3,96,384]{2,1,0:T(8,128)}, f32[96,384]{1,0:T(8,128)}, f32[3,64,3312]{2,1,0:T(8,128)}, bf16[6,12,8,96]{3,2,1,0:T(8,128)(2,1)}) custom-call(s32[1]{0:T(128)S(6)} %copy.21.shift_ref, bf16[8,48,384]{2,1,0:T(8,128)(2,1)S(1)} %get-tuple-element.54.sums, bf16[8,8,16,256]{3,2,1,0:T(8,128)(2,1)S(1)} %get-tuple-element.55.folded, ...), custom_call_target="tpu_custom_call" | custom-call | tf_op jit(solution)/shard_map/finish/pallas_call | solution.py:483

commit v3 on v2

v3 whole, which is shorter than its diff:
```python
import functools

import jax
import jax.numpy as jnp
from jax import lax
from jax.experimental import pallas as pl
from jax.experimental.pallas import tpu as pltpu
from jax.sharding import PartitionSpec as P

F32 = jnp.float32
BF16 = jnp.bfloat16
HEADS = 3
WINS = 4
WIDTH = 96
HEAD = 32
SLOTS = 12
GRID = 72
TOKENS = 144
MODEL = 384
SPAN = 23
TABLE = 3312
TABLE_PAD = 3328
GROUP = 138
SCALE = HEAD ** (-0.5)
VMEM = pl.BlockSpec(memory_space=pltpu.VMEM)
SMEM = pl.BlockSpec(memory_space=pltpu.SMEM)
ANY = pl.BlockSpec(memory_space=pl.ANY)


def dot(a, b, da, db):
    return lax.dot_general(a, b, (((da,), (db,)), ((), ())), preferred_element_type=F32)


def three(x):
    hi = x.astype(BF16)
    rest = x - hi.astype(F32)
    mid = rest.astype(BF16)
    return hi, mid, (rest - mid.astype(F32)).astype(BF16)


def fold_map(ci, shift):
    rows = lax.broadcasted_iota(jnp.int32, (288, 256), 0)
    lane = lax.broadcasted_iota(jnp.int32, (1, 256), 1)
    block = lane // SLOTS
    cj = lane - block * SLOTS
    wrap = jnp.where(ci < shift, 12, 0) - jnp.where(cj < shift, 12, 0)
    target = block * SPAN + (11 + ci) - cj + wrap
    target = jnp.where(lane < TOKENS, target, -1)
    return jnp.where(rows == target, 1.0, 0.0).astype(BF16)


def expand_bias(types, shift, table, tabw, spread, maps, bias):
    for h in range(HEADS):
        for w in range(WINS):
            n = h * WINS + w
            tabw[n : n + 1, 0:TABLE] = table[h, pl.ds(types[w], 1), :]
    spread[...] = jnp.zeros_like(spread)
    for zi in range(2):
        for ai in range(6):
            for zj in range(2):
                at = zi * 1656 + zj * 828 + ai * GROUP
                spread[zi * 6 + ai, 0:12, zj * GROUP : (zj + 1) * GROUP] = tabw[0:12, at : at + GROUP]
    parts = three(spread[...].reshape(192, 288))
    for ci in range(SLOTS):
        chosen = fold_map(ci, shift)
        maps[ci] = chosen
        full = dot(parts[0], chosen, 1, 0) + dot(parts[1], chosen, 1, 0) + dot(parts[2], chosen, 1, 0)
        for n in range(12):
            for k in range(2):
                bias[k, pl.ds(n * SLOTS + ci, 12, stride=TOKENS), :] = full[
                    n * 16 : n * 16 + 12, k * 128 : (k + 1) * 128
                ]


def window_rows(scratch, w):
    halves = []
    for z in range(2):
        lanes = [scratch[k, pl.ds(2 * w + z, GRID, stride=8), :] for k in range(3)]
        halves.append(jnp.concatenate(lanes, axis=1))
    return jnp.concatenate(halves, axis=0).astype(BF16)


def place_rows(own, borrowed, shift, scratch, first, slots):
    for c in slots:
        for a in range(6):
            rows = own[a, c].astype(F32)
            if borrowed is not None:
                keep = c >= shift if first == 0 else c < shift
                rows = jnp.where(keep, rows, borrowed[a, c - first].astype(F32))
            for k in range(3):
                scratch[k, (a * SLOTS + c) * 8 : (a * SLOTS + c + 1) * 8, :] = rows[:, k * 128 : (k + 1) * 128]


def only(x, h):
    return jnp.concatenate([x[k * HEAD : (k + 1) * HEAD] if k == h else jnp.zeros((HEAD, x.shape[1]), x.dtype) for k in range(HEADS)], axis=0)


def forward(xs, wts, bias, proj_out, softs, atts):
    tops = {}
    for w in range(WINS):
        xw = window_rows(xs, w)
        proj = dot(wts, xw, 1, 1).astype(BF16)
        proj_out[w] = proj
        q = dot(xw, wts[0:WIDTH], 1, 1).astype(BF16)
        for h in range(HEADS):
            n = h * WINS + w
            rows = slice(n * TOKENS, (n + 1) * TOKENS)
            added = jnp.concatenate([bias[0, rows, :], bias[1, rows, 0:16]], axis=1)
            logits = dot(q, only(proj[96:192], h), 1, 0) * SCALE + added
            softs[n] = logits
            tops[n] = jnp.max(logits, axis=1, keepdims=True)
    for w in range(WINS):
        sums = []
        for h in range(HEADS):
            n = h * WINS + w
            raised = jnp.exp(softs[n] - tops[n])
            softs[n] = raised
            sums.append(1.0 / jnp.sum(raised, axis=1, keepdims=True))
        att = []
        for h in range(HEADS):
            n = h * WINS + w
            soft = softs[n] * sums[h]
            softs[n] = soft
            att.append(dot(proj_out[w, 192 + h * HEAD : 192 + (h + 1) * HEAD, :], soft.astype(BF16), 1, 1))
        atts[w] = jnp.concatenate(att, axis=0).astype(BF16)


def backward(xs, gs, wos, proj_in, softs, gsofts, atts, scores, sums, dprojs):
    rowsums, dats = {}, {}
    for w in range(WINS):
        gw = window_rows(gs, w)
        dats[w] = dot(wos, gw, 1, 1).astype(BF16)
        da = dot(gw, wos, 1, 1).astype(BF16)
        vt = proj_in[w, 192:288, :]
        for h in range(HEADS):
            n = h * WINS + w
            gsoft = dot(da, only(vt, h), 1, 0)
            gsofts[n] = gsoft
            rowsums[n] = jnp.sum(softs[n] * gsoft, axis=1, keepdims=True)
        low = dot(atts[w], gw, 1, 0)
        if w == 0:
            sums[288:384, :] = low
        else:
            sums[288:384, :] += low
    for w in range(WINS):
        dq, dk, dv = [], [], []
        for h in range(HEADS):
            n = h * WINS + w
            rows = slice(n * TOKENS, (n + 1) * TOKENS)
            own = slice(h * HEAD, (h + 1) * HEAD)
            soft = softs[n]
            gsc = soft * (gsofts[n] - rowsums[n])
            scores[0, rows, :] = gsc[:, 0:128]
            scores[1, rows, 0:16] = gsc[:, 128:144]
            gh = gsc.astype(BF16)
            dv.append(dot(dats[w][own], soft.astype(BF16), 1, 0))
            dq.append(dot(proj_in[w, 96 + h * HEAD : 96 + (h + 1) * HEAD, :], gh, 1, 1) * SCALE)
            dk.append(dot(proj_in[w, own, :], gh, 1, 0) * SCALE)
        dproj = jnp.concatenate(dq + dk + dv, axis=0).astype(BF16)
        dprojs[w] = dproj
        top = dot(dproj, window_rows(xs, w), 1, 0)
        if w == 0:
            sums[0:288, :] = top
        else:
            sums[0:288, :] += top


def fold_scores(types, scores, maps, fold, folded, folded_out):
    total = None
    for ci in range(SLOTS):
        part = jnp.concatenate(
            [scores[0, pl.ds(ci, TOKENS, stride=SLOTS), :], scores[1, pl.ds(ci, TOKENS, stride=SLOTS), :][:, 0:16]], axis=1
        )
        term = dot(part.astype(BF16), maps[ci][:, 0:TOKENS], 1, 1)
        total = term if total is None else total + term
    for k in range(3):
        wide = min(128, 288 - k * 128)
        fold[k, :, 0:wide] = total[:, k * 128 : k * 128 + wide]
    folded[...] = jnp.zeros_like(folded)
    for zi in range(2):
        for ai in range(6):
            got = [fold[k, pl.ds(zi * 6 + ai, 12, stride=12), :] for k in range(3)]
            line = jnp.concatenate(got, axis=1)
            for zj in range(2):
                at = zi * 1656 + zj * 828 + ai * GROUP
                folded[0:12, at : at + GROUP] = line[:, zj * GROUP : (zj + 1) * GROUP]
    row = lax.broadcasted_iota(jnp.int32, (16, 256), 0)
    marks = jnp.zeros((16, 256), jnp.int32)
    for w in range(WINS):
        marks = jnp.where(row == 12 + w, types[w], marks)
    marks = marks.astype(F32)
    for z in range(16):
        part = folded[:, z * 256 : (z + 1) * 256]
        folded_out[z] = jnp.where(row < 12, part, marks).astype(BF16)


def pieces_out(wflip, dprojs, piece):
    for w in range(WINS):
        back = dot(wflip[...], dprojs[w], 1, 0).astype(BF16)
        for r in range(4):
            piece[r, :, w * TOKENS : (w + 1) * TOKENS] = back[r * WIDTH : (r + 1) * WIDTH]
    for r in range(4):
        piece[r, :, 576:640] = jnp.zeros((WIDTH, 64), BF16)


def pick_types(lines):
    marks = jnp.concatenate([lines[q][12:16, 0:1] for q in range(4)], axis=0) * 0.0625
    lane = lax.broadcasted_iota(jnp.int32, (16, 128), 1).astype(F32)
    return jnp.where(lane == marks, 1.0, 0.0).T[0:64].astype(BF16)


def finish_kernel(shift_ref, sums, folded, own, far, attend_out, output_out, bias_out, feat_out):
    whole = [
        jnp.concatenate([folded[xh * 4 + q, z] for z in range(7) for xh in range(2)], axis=1).astype(F32) for q in range(4)
    ]
    pick = pick_types(whole)
    for h in range(HEADS):
        rows = jnp.concatenate([whole[q][h * WINS : (h + 1) * WINS, 0:TABLE_PAD] for q in range(4)], axis=0)
        bias_out[h] = dot(pick, rows.astype(BF16), 1, 0)[:, 0:TABLE]
    for i in range(8):
        for r in range(3):
            for k in range(3):
                part = sums[i, r * 3 + k].astype(F32)
                at, lanes = (i % 2) * 48 + r * 16, slice(k * 128, (k + 1) * 128)
                if i < 6:
                    attend_out[i // 2, at : at + 16, lanes] = part
                else:
                    output_out[at : at + 16, lanes] = part
    shift = shift_ref[0]
    for c in range(SLOTS):
        mine = jnp.where(shift <= 6, c - shift, shift - 1 - c) >= 0
        for a in range(6):
            feat_out[a, c] = jnp.where(mine, own[a, c].astype(F32), far[a, c % 6].astype(F32)).astype(BF16)[:, 0:WIDTH]


def place_features(feat, lines, out):
    for w in range(WINS):
        both = jnp.concatenate([feat[:, w * TOKENS : (w + 1) * TOKENS], jnp.zeros((32, TOKENS), F32)], axis=0).T
        for z in range(2):
            lines[pl.ds(2 * w + z, GRID, stride=8), :] = both[z * GRID : (z + 1) * GRID]
    for a in range(6):
        for c in range(SLOTS):
            at = (a * SLOTS + c) * 8
            out[a, c] = lines[at : at + 8, :].astype(BF16)


class Links:
    def __init__(self, send, recv):
        self.send, self.recv, self.used, self.sent = send, recv, 0, []

    def copy(self, src, dst, to):
        k = self.used
        self.used += 1
        return pltpu.make_async_remote_copy(
            src_ref=src,
            dst_ref=dst,
            send_sem=self.send.at[k],
            recv_sem=self.recv.at[k],
            device_id=to,
            device_id_type=pl.DeviceIdType.MESH,
        )

    def start(self, src, dst, to):
        made = self.copy(src, dst, to)
        made.start()
        self.sent.append(made)
        return made

    def settle(self):
        for made in self.sent:
            made.wait_send()
        self.sent = []


def place():
    lon, lat, head = lax.axis_index("lon"), lax.axis_index("lat"), lax.axis_index("head")
    z, high = lon // 2, lon % 2
    low, core = lat // 2, lat % 2
    return lon, lat, head, z, high, high * 2 + low, core


def at_grid(z, x, core):
    return {"lon": z * 2 + x // 2, "lat": (x % 2) * 2 + core}


def greet(peers):
    barrier = pltpu.get_barrier_semaphore()
    for peer in peers:
        pl.semaphore_signal(barrier, inc=1, device_id=peer, device_id_type=pl.DeviceIdType.MESH)
    return len(peers)


def reduce_peers():
    lon, lat, head, z, high, x, core = place()
    xc = x * 2 + core
    peers = [{"lon": (lon + k) % 16} for k in range(1, 16)]
    peers += [at_grid(z, ((xc + k) % 8) // 2, (xc + k) % 2) for k in range(1, 8)]
    peers += [{"head": (head + k) % 4} for k in range(1, 4)]
    return peers


NAMES = dict(
    xv=pltpu.VMEM((6, SLOTS, 8, MODEL), BF16),
    gv=pltpu.VMEM((6, SLOTS, 8, MODEL), BF16),
    xe=pltpu.VMEM((6, 6, 8, MODEL), BF16),
    ge=pltpu.VMEM((6, 6, 8, MODEL), BF16),
    tabv=pltpu.VMEM((3, 64, TABLE), F32),
    wtv=pltpu.VMEM((3, WIDTH, MODEL), BF16),
    wov=pltpu.VMEM((WIDTH, MODEL), BF16),
    tabw=pltpu.VMEM((16, TABLE_PAD), F32),
    spread=pltpu.VMEM((12, 16, 288), F32),
    maps=pltpu.VMEM((12, 288, 256), BF16),
    bias=pltpu.VMEM((2, 1728, 128), F32),
    xs=pltpu.VMEM((3, 576, 128), F32),
    gs=pltpu.VMEM((3, 576, 128), F32),
    wflip=pltpu.VMEM((MODEL, 288), BF16),
    projs=pltpu.VMEM((WINS, 288, TOKENS), BF16),
    gsofts=pltpu.VMEM((12, TOKENS, TOKENS), F32),
    softs=pltpu.VMEM((12, TOKENS, TOKENS), F32),
    atts=pltpu.VMEM((WINS, WIDTH, TOKENS), BF16),
    scores=pltpu.VMEM((2, 1728, 128), F32),
    dprojs=pltpu.VMEM((WINS, 288, TOKENS), BF16),
    fold=pltpu.VMEM((3, TOKENS, 128), F32),
    sums=pltpu.VMEM((MODEL, MODEL), F32),
    folded=pltpu.VMEM((16, 4096), F32),
    a0=pltpu.VMEM((4, 48, MODEL), BF16),
    ad=pltpu.VMEM((4, 48, MODEL), BF16),
    ax=pltpu.VMEM((4, 48, MODEL), BF16),
    f0=pltpu.VMEM((16, 16, 256), BF16),
    p0=pltpu.VMEM((4, WIDTH, 640), BF16),
    a1=pltpu.VMEM((3, 48, MODEL), BF16),
    f1=pltpu.VMEM((15, 16, 256), BF16),
    p1=pltpu.VMEM((3, WIDTH, 640), BF16),
    a2s=pltpu.VMEM((8, 2, 16, 128), BF16),
    a2=pltpu.VMEM((7, 2, 16, 128), BF16),
    a3=pltpu.VMEM((8, 16, 128), BF16),
    lines=pltpu.VMEM((576, 128), F32),
    f3=pltpu.VMEM((8, 16, 256), BF16),
    send=pltpu.SemaphoreType.DMA((72,)),
    recv=pltpu.SemaphoreType.DMA((72,)),
    load=pltpu.SemaphoreType.DMA((8,)),
    types=pltpu.SMEM((1, 4), jnp.int32),
    shift=pltpu.SMEM((1,), jnp.int32),
)


def main_kernel(first, types_ref, shift_ref, x, g, table, wt, wo, a_out, f_out, own_out, west_out, *scratch):
    v = dict(zip(NAMES, scratch, strict=True))
    lon, lat, head, z, high, xpos, core = place()
    xc = xpos * 2 + core
    step = 1 if first == 0 else 15
    net = Links(v["send"], v["recv"])
    met = greet(reduce_peers())
    loads = []
    given = ((types_ref, "types"), (shift_ref, "shift"), (table, "tabv"), (x, "xv"), (g, "gv"), (wt, "wtv"), (wo, "wov"))
    for src, dst in given:
        made = pltpu.make_async_copy(src, v[dst], v["load"].at[len(loads)])
        made.start()
        loads.append(made)
    with jax.named_scope("bias"):
        for made in loads[0:3]:
            made.wait()
        types = [v["types"][0, w] for w in range(WINS)]
        shift = v["shift"][0]
        expand_bias(types, shift, v["tabv"], v["tabw"], v["spread"], v["maps"], v["bias"])
    with jax.named_scope("enter"):
        for made in loads[3:5]:
            made.wait()
        pl.semaphore_wait(pltpu.get_barrier_semaphore(), met)

    giver = {"lon": (lon + 16 - step) % 16}
    rows, cols = pl.ds((head // 2) * 3, 3), (head % 2) * 3
    quarter = v["ge"].at[rows, pl.ds(cols, 3)]
    halo = [net.start(v["gv"].at[rows, pl.ds(first + cols, 3)], quarter, giver)]
    halo.append(net.start(v["xv"].at[:, pl.ds(first, 6)], v["xe"], giver))
    mixed = [c for c in range(first, first + 6)]
    still = [c for c in range(SLOTS) if c not in mixed]
    place_rows(v["xv"], None, shift, v["xs"], first, still)
    place_rows(v["gv"], None, shift, v["gs"], first, still)
    with jax.named_scope("still"):
        loads[5].wait()
        loads[6].wait()
        wts = v["wtv"][...].reshape(3 * WIDTH, MODEL)
        wos = v["wov"][...]
        v["wflip"][...] = wts.astype(F32).T.astype(BF16)

    with jax.named_scope("halo_q"):
        halo[0].wait_recv()
    handed = [net.start(quarter, quarter, {"head": (head + j) % 4}) for j in range(1, 4)]
    with jax.named_scope("halo_x"):
        halo[1].wait_recv()
    with jax.named_scope("forward"):
        place_rows(v["xv"], v["xe"], shift, v["xs"], first, mixed)
        forward(v["xs"], wts, v["bias"], v["projs"], v["softs"], v["atts"])
    with jax.named_scope("halo_g"):
        for made in handed:
            made.wait_recv()
    with jax.named_scope("backward"):
        place_rows(v["gv"], v["ge"], shift, v["gs"], first, mixed)
        backward(v["xs"], v["gs"], wos, v["projs"], v["softs"], v["gsofts"], v["atts"], v["scores"], v["sums"], v["dprojs"])

    def zs(k):
        return {"lon": ((z + k) % 8) * 2 + high}

    a0, f0, p0 = v["a0"], v["f0"], v["p0"]
    a1, f1, p1 = v["a1"], v["f1"], v["p1"]
    ad, ax, a2s, a2, a3, f3 = (v[n] for n in ("ad", "ax", "a2s", "a2", "a3", "f3"))
    partner = at_grid(z, xpos, 1 - core)

    def chunk(i, side):
        return v["sums"][pl.ds(pl.multiple_of((2 * i + side) * 48, 16), 48), :]

    for i in range(4):
        a0[i] = chunk(i, 1 - core).astype(BF16)
    twin = net.start(a0, ad, partner)
    with jax.named_scope("fold"):
        fold_scores(types, v["scores"], v["maps"], v["fold"], v["folded"], f0)
    with jax.named_scope("sum_d"):
        twin.wait_recv()
        for i in range(4):
            ax[i] = (chunk(i, core) + ad[i].astype(F32)).astype(BF16)
    one = [net.start(ax.at[(xpos + k) % 4], a1.at[k - 1], at_grid(z, (xpos + k) % 4, core)) for k in range(1, 4)]
    two = [net.start(f0.at[(lon + k) % 16], f1.at[k - 1], {"lon": (lon + k) % 16}) for k in range(1, 16)]
    with jax.named_scope("pieces"):
        pieces_out(v["wflip"], v["dprojs"], p0)
    pieces = [net.start(p0.at[(head + k) % 4], p1.at[k - 1], {"head": (head + k) % 4}) for k in range(1, 4)]

    with jax.named_scope("sum_a"):
        total = chunk(xpos, core) + ad[xpos].astype(F32)
        for k in range(3):
            one[k].wait_recv()
            total = total + a1[k].astype(F32)
        tiles = [total[r * 16 : (r + 1) * 16, k * 128 : (k + 1) * 128].astype(BF16) for r in range(3) for k in range(3)]
        for k in range(8):
            a2s[k, 0] = tiles[k]
            a2s[k, 1] = tiles[8]
    three_ = [net.start(a2s.at[(z + k) % 8], a2.at[k - 1], zs(k)) for k in range(1, 8)]

    with jax.named_scope("sum_f"):
        lines = f0[lon].astype(F32)
        for k in range(15):
            two[k].wait_recv()
            lines = lines + f1[k].astype(F32)
        f3[z] = lines.astype(BF16)
    five = [net.start(f3.at[z], f3.at[z], zs(k)) for k in range(1, 8)]

    with jax.named_scope("sum_z"):
        block = a2s[z].astype(F32)
        for k in range(7):
            three_[k].wait_recv()
            block = block + a2[k].astype(F32)
        a3[z] = block[0].astype(BF16)
    six = [net.start(a3.at[z], a3.at[z], zs(k)) for k in range(1, 8)]
    a_out[xc, 8] = block[1].astype(BF16)

    with jax.named_scope("sum_p"):
        feat = p0[head].astype(F32)
        for k in range(3):
            pieces[k].wait_recv()
            feat = feat + p1[k].astype(F32)
        place_features(feat, v["lines"], own_out)
    net.settle()
    back = net.start(own_out.at[:, pl.ds(first, 6)], west_out, {"lon": (lon + step) % 16})

    with jax.named_scope("all_f"):
        for k in range(7):
            five[k].wait_recv()
    part = f3.at[pl.ds(0, 7)]
    mine = f_out.at[xc, pl.ds(0, 7)]
    arrive_f = [net.start(part, mine, at_grid(z, (xpos + k) % 4, core)) for k in range(1, 4)]
    cross = [net.start(part, mine, partner)]
    f_out[xc] = f3[...]
    with jax.named_scope("all_a"):
        for k in range(7):
            six[k].wait_recv()
    a_out[xc, 0:8] = a3[...]
    arrive = [net.start(a_out.at[xc], a_out.at[xc], at_grid(z, (xpos + k) % 4, core)) for k in range(1, 4)]
    cross.append(net.start(a_out.at[xc], a_out.at[xc], partner))
    with jax.named_scope("forward_x"):
        for arrived, out, whole in ((arrive_f, f_out, False), (arrive, a_out, True)):
            for k in range(1, 4):
                there = ((xpos + 4 - k) % 4) * 2 + core
                arrived[k - 1].wait_recv()
                ref = out.at[there] if whole else out.at[there, pl.ds(0, 7)]
                cross.append(net.start(ref, ref, partner))
    net.settle()
    with jax.named_scope("last"):
        back.wait_recv()
        for made in cross:
            made.wait_recv()


def per_device(features, attend_weight, output_weight, bias_table, bias_type, window_shift, grad_out):
    x = features.transpose(1, 2, 0, 3)
    g = grad_out.transpose(1, 2, 0, 3)
    wt = attend_weight.transpose(0, 2, 1)
    table = bias_table.transpose(1, 0, 2)

    def run(first):
        return pl.pallas_call(
            functools.partial(main_kernel, first),
            out_shape=(
                jax.ShapeDtypeStruct((8, 9, 16, 128), BF16),
                jax.ShapeDtypeStruct((8, 8, 16, 256), BF16),
                jax.ShapeDtypeStruct((6, SLOTS, 8, 128), BF16),
                jax.ShapeDtypeStruct((6, 6, 8, 128), BF16),
            ),
            in_specs=[ANY] * 7,
            out_specs=(VMEM,) * 4,
            scratch_shapes=list(NAMES.values()),
            compiler_params=pltpu.CompilerParams(
                vmem_limit_bytes=56 << 20, collective_id=1 if first == 0 else 2, has_side_effects=True
            ),
            name="block_east" if first == 0 else "block_west",
        )

    args = (bias_type.T, window_shift, x, g, table, wt, output_weight)
    sums, folded, own, borrowed = lax.cond(window_shift[0] <= 6, run(0), run(6), *args)
    return finish(window_shift, sums, folded, own, borrowed)


def finish(window_shift, sums, folded, own, borrowed):
    attend_grad, output_grad, bias_grad, feat = pl.pallas_call(
        finish_kernel,
        out_shape=(
            jax.ShapeDtypeStruct((3, WIDTH, MODEL), F32),
            jax.ShapeDtypeStruct((WIDTH, MODEL), F32),
            jax.ShapeDtypeStruct((3, 64, TABLE), F32),
            jax.ShapeDtypeStruct((6, SLOTS, 8, WIDTH), BF16),
        ),
        in_specs=[SMEM, VMEM, VMEM, VMEM, VMEM],
        out_specs=(VMEM,) * 4,
        compiler_params=pltpu.CompilerParams(vmem_limit_bytes=40 << 20),
        name="finish",
    )(window_shift, sums, folded, own, borrowed)
    return (
        feat.transpose(2, 0, 1, 3),
        attend_grad.transpose(0, 2, 1),
        output_grad,
        bias_grad.transpose(1, 0, 2),
    )


def solution(mesh):
    placed = (
        P(None, "lat", "lon", None),
        P(None, None, "head"),
        P("head", None),
        P(None, "head", None),
        P(None, "lat"),
        P(),
        P(None, "lat", "lon", None),
    )
    return jax.shard_map(
        per_device,
        mesh=mesh,
        in_specs=placed,
        out_specs=(
            P(None, "lat", "lon", "head"),
            P(None, None, "head"),
            P("head", None),
            P(None, "head", None),
        ),
        check_vma=False,
    )
```

time: 61.5 us -> 52.9 us (0.86)
  Pallas kernels: 58.5 us -> 51.3 us
  local copies, waits for them, and re-layouts: 1.31 us -> 0 us
    pallas_call x1, Pallas kernels: 56.3 us -> 49 us  [per_device(): lax.cond(window_shift[0] <= 6, run(0), run(6), *args)]
    another operation x1 -> x0, local copies, waits for them, and re-layouts: 1.31 us -> none
where the time goes in v3:
time: 52.9 us; the launch traced here: 52.8 us
  Pallas kernels  51.3 us (97%)
  between operations  1.29 us (2%)
    pallas_call x1, Pallas kernels, per_device(): lax.cond(window_shift[0] <= 6, run(0), run(6), *args)  49 us
    pallas_call x1, Pallas kernels, finish(): pl.pallas_call(finish_kernel, out_shape=(jax.ShapeDtypeStruct((3, WIDTH,...  2.28 us

profile of v3, /device:TPU:1, one launch (start us, length us, event | category | flops | bytes accessed | tf_op | source)
XLA Modules:
  0.0 52.8 jit_solution(14064276431466243228)
XLA Ops:
  1.3 49.2 %conditional.1 = ((bf16[8,9,16,128]{3,2,1,0:T(8,128)(2,1)S(1)}, bf16[8,8,16,256]{3,2,1,0:T(8,128)(2,1)S(1)}, bf16[6,12,8,128]{3,2,1,0:T(8,128)(2,1)S(1)}, bf16[6,6,8,128]{3,2,1,0:T(8,128)(2,1)S(1)})) conditional(s32[]{:T(128)} %bitcast, (s32[1,4]{1,0:T(1,128)}, s32[1]{0:T(128)}, bf16[6,12,8,384]{3,2,1,0:T(8,128)(2,1)}, ...), branch_computations={%region_0.0_spmd, %region_1.0_spmd} | conditional | bytes 8 | solution.py:518
  1.3 49.0 %block_west.1 = (bf16[8,9,16,128]{3,2,1,0:T(8,128)(2,1)S(1)}, bf16[8,8,16,256]{3,2,1,0:T(8,128)(2,1)S(1)}, bf16[6,12,8,128]{3,2,1,0:T(8,128)(2,1)S(1)}, bf16[6,6,8,128]{3,2,1,0:T(8,128)(2,1)S(1)}) custom-call(s32[1,4]{1,0:T(1,128)} %get-tuple-element.28.types_ref, s32[1]{0:T(128)} %get-tuple-element.29.shift_ref, ...), custom_call_target="tpu_custom_call" | custom-call | tf_op jit(solution)/shard_map/cond/branch_0_fun/block_west/pallas_call | solution.py:518
  50.5 2.3 %finish.1 = (f32[3,96,384]{2,1,0:T(8,128)}, f32[96,384]{1,0:T(8,128)}, f32[3,64,3312]{2,1,0:T(8,128)}, bf16[6,12,8,96]{3,2,1,0:T(8,128)(2,1)}) custom-call(s32[1]{0:T(128)S(6)} %copy.19.shift_ref, bf16[8,9,16,128]{3,2,1,0:T(8,128)(2,1)S(1)} %get-tuple-element.54.sums, bf16[8,8,16,256]{3,2,1,0:T(8,128)(2,1)S(1)} %get-tuple-element.55.folded, ...), custom_call_target="tpu_custom_call" | custom-call | tf_op jit(solution)/shard_map/finish/pallas_call | solution.py:523

commit v4 on v3

--- a/solution.py
+++ b/solution.py
@@ -184,14 +184,17 @@
             for zj in range(2):
                 at = zi * 1656 + zj * 828 + ai * GROUP
                 folded[0:12, at : at + GROUP] = line[:, zj * GROUP : (zj + 1) * GROUP]
-    row = lax.broadcasted_iota(jnp.int32, (16, 256), 0)
-    marks = jnp.zeros((16, 256), jnp.int32)
-    for w in range(WINS):
-        marks = jnp.where(row == 12 + w, types[w], marks)
-    marks = marks.astype(F32)
-    for z in range(16):
-        part = folded[:, z * 256 : (z + 1) * 256]
-        folded_out[z] = jnp.where(row < 12, part, marks).astype(BF16)
+    row = lax.broadcasted_iota(jnp.int32, (16, 128), 0)
+    lane = lax.broadcasted_iota(jnp.int32, (16, 128), 1)
+    marks = jnp.zeros((16, 128), jnp.int32)
+    for w in range(WINS):
+        marks = jnp.where(row == w, types[w], marks)
+    folded[:, 3200:TABLE_PAD] = jnp.where(lane >= 112, marks.astype(F32), folded[:, 3200:TABLE_PAD])
+    for i in range(16):
+        left, right = (folded[:, i * 256 + k * 128 : i * 256 + (k + 1) * 128] for k in range(2))
+        folded_out[i, 0] = left[0:8].astype(BF16)
+        folded_out[i, 1] = right[0:8].astype(BF16)
+        folded_out[i, 2] = jnp.concatenate([left[8:12], right[8:12]], axis=0).astype(BF16)
 
 
 def pieces_out(wflip, dprojs, piece):
@@ -203,20 +206,23 @@
         piece[r, :, 576:640] = jnp.zeros((WIDTH, 64), BF16)
 
 
-def pick_types(lines):
-    marks = jnp.concatenate([lines[q][12:16, 0:1] for q in range(4)], axis=0) * 0.0625
+def finish_kernel(shift_ref, sums, folded, own, far, attend_out, output_out, bias_out, feat_out):
+    first, last = [], []
+    for q in range(4):
+        high, low = [], []
+        for z in range(7):
+            for xh in range(2):
+                part = folded[xh * 4 + q, z].astype(F32)
+                high += [part[0], part[1]]
+                low += [part[2, 0:4], part[2, 4:8]]
+        first.append(jnp.concatenate(high[0:26], axis=1))
+        last.append(jnp.concatenate(low[0:26], axis=1))
+    marks = jnp.concatenate([first[q][0:4, TABLE : TABLE + 1] for q in range(4)], axis=0) * 0.0625
     lane = lax.broadcasted_iota(jnp.int32, (16, 128), 1).astype(F32)
-    return jnp.where(lane == marks, 1.0, 0.0).T[0:64].astype(BF16)
-
-
-def finish_kernel(shift_ref, sums, folded, own, far, attend_out, output_out, bias_out, feat_out):
-    whole = [
-        jnp.concatenate([folded[xh * 4 + q, z] for z in range(7) for xh in range(2)], axis=1).astype(F32) for q in range(4)
-    ]
-    pick = pick_types(whole)
+    pick = jnp.where(lane == marks, 1.0, 0.0).T[0:64].astype(BF16)
     for h in range(HEADS):
-        rows = jnp.concatenate([whole[q][h * WINS : (h + 1) * WINS, 0:TABLE_PAD] for q in range(4)], axis=0)
-        bias_out[h] = dot(pick, rows.astype(BF16), 1, 0)[:, 0:TABLE]
+        rows = [first[q][h * WINS : (h + 1) * WINS] if h < 2 else last[q] for q in range(4)]
+        bias_out[h] = dot(pick, jnp.concatenate(rows, axis=0).astype(BF16), 1, 0)[:, 0:TABLE]
     for i in range(8):
         for r in range(3):
             for k in range(3):
@@ -248,9 +254,11 @@
     def __init__(self, send, recv):
         self.send, self.recv, self.used, self.sent = send, recv, 0, []
 
-    def copy(self, src, dst, to):
-        k = self.used
+    def slot(self):
         self.used += 1
+        return self.used - 1
+
+    def copy(self, k, src, dst, to):
         return pltpu.make_async_remote_copy(
             src_ref=src,
             dst_ref=dst,
@@ -260,11 +268,23 @@
             device_id_type=pl.DeviceIdType.MESH,
         )
 
-    def start(self, src, dst, to):
-        made = self.copy(src, dst, to)
+    def start(self, src, dst, to, k=None):
+        made = self.copy(self.slot() if k is None else k, src, dst, to)
         made.start()
+        if k is None:
+            self.sent.append(made)
+        return made
+
+    def group(self, k, whole, to):
+        made = self.copy(k, whole, whole, to)
         self.sent.append(made)
         return made
+
+    def many(self, whole, moves):
+        k = self.slot()
+        for src, dst, to in moves:
+            self.start(src, dst, to, k)
+        return self.group(k, whole, moves[-1][2])
 
     def settle(self):
         for made in self.sent:
@@ -326,19 +346,19 @@
     a0=pltpu.VMEM((4, 48, MODEL), BF16),
     ad=pltpu.VMEM((4, 48, MODEL), BF16),
     ax=pltpu.VMEM((4, 48, MODEL), BF16),
-    f0=pltpu.VMEM((16, 16, 256), BF16),
+    f0=pltpu.VMEM((16, 3, 8, 128), BF16),
     p0=pltpu.VMEM((4, WIDTH, 640), BF16),
     a1=pltpu.VMEM((3, 48, MODEL), BF16),
-    f1=pltpu.VMEM((15, 16, 256), BF16),
+    f1=pltpu.VMEM((15, 3, 8, 128), BF16),
     p1=pltpu.VMEM((3, WIDTH, 640), BF16),
     a2s=pltpu.VMEM((8, 2, 16, 128), BF16),
     a2=pltpu.VMEM((7, 2, 16, 128), BF16),
     a3=pltpu.VMEM((8, 16, 128), BF16),
     lines=pltpu.VMEM((576, 128), F32),
-    f3=pltpu.VMEM((8, 16, 256), BF16),
-    send=pltpu.SemaphoreType.DMA((72,)),
-    recv=pltpu.SemaphoreType.DMA((72,)),
-    load=pltpu.SemaphoreType.DMA((8,)),
+    f3=pltpu.VMEM((8, 3, 8, 128), BF16),
+    send=pltpu.SemaphoreType.DMA((21,)),
+    recv=pltpu.SemaphoreType.DMA((21,)),
+    load=pltpu.SemaphoreType.DMA((7,)),
     types=pltpu.SMEM((1, 4), jnp.int32),
     shift=pltpu.SMEM((1,), jnp.int32),
 )
@@ -352,19 +372,13 @@
     net = Links(v["send"], v["recv"])
     met = greet(reduce_peers())
     loads = []
-    given = ((types_ref, "types"), (shift_ref, "shift"), (table, "tabv"), (x, "xv"), (g, "gv"), (wt, "wtv"), (wo, "wov"))
+    given = ((g, "gv"), (x, "xv"), (types_ref, "types"), (shift_ref, "shift"), (table, "tabv"), (wt, "wtv"), (wo, "wov"))
     for src, dst in given:
         made = pltpu.make_async_copy(src, v[dst], v["load"].at[len(loads)])
         made.start()
         loads.append(made)
-    with jax.named_scope("bias"):
-        for made in loads[0:3]:
-            made.wait()
-        types = [v["types"][0, w] for w in range(WINS)]
-        shift = v["shift"][0]
-        expand_bias(types, shift, v["tabv"], v["tabw"], v["spread"], v["maps"], v["bias"])
     with jax.named_scope("enter"):
-        for made in loads[3:5]:
+        for made in loads[0:2]:
             made.wait()
         pl.semaphore_wait(pltpu.get_barrier_semaphore(), met)
 
@@ -373,6 +387,12 @@
     quarter = v["ge"].at[rows, pl.ds(cols, 3)]
     halo = [net.start(v["gv"].at[rows, pl.ds(first + cols, 3)], quarter, giver)]
     halo.append(net.start(v["xv"].at[:, pl.ds(first, 6)], v["xe"], giver))
+    with jax.named_scope("bias"):
+        for made in loads[2:5]:
+            made.wait()
+        types = [v["types"][0, w] for w in range(WINS)]
+        shift = v["shift"][0]
+        expand_bias(types, shift, v["tabv"], v["tabw"], v["spread"], v["maps"], v["bias"])
     mixed = [c for c in range(first, first + 6)]
     still = [c for c in range(SLOTS) if c not in mixed]
     place_rows(v["xv"], None, shift, v["xs"], first, still)
@@ -419,70 +439,73 @@
         twin.wait_recv()
         for i in range(4):
             ax[i] = (chunk(i, core) + ad[i].astype(F32)).astype(BF16)
-    one = [net.start(ax.at[(xpos + k) % 4], a1.at[k - 1], at_grid(z, (xpos + k) % 4, core)) for k in range(1, 4)]
-    two = [net.start(f0.at[(lon + k) % 16], f1.at[k - 1], {"lon": (lon + k) % 16}) for k in range(1, 16)]
+    one = net.many(a1, [(ax.at[(xpos + k) % 4], a1.at[k - 1], at_grid(z, (xpos + k) % 4, core)) for k in range(1, 4)])
+    two = net.many(f1, [(f0.at[(lon + k) % 16], f1.at[k - 1], {"lon": (lon + k) % 16}) for k in range(1, 16)])
     with jax.named_scope("pieces"):
         pieces_out(v["wflip"], v["dprojs"], p0)
-    pieces = [net.start(p0.at[(head + k) % 4], p1.at[k - 1], {"head": (head + k) % 4}) for k in range(1, 4)]
+    pieces = net.many(p1, [(p0.at[(head + k) % 4], p1.at[k - 1], {"head": (head + k) % 4}) for k in range(1, 4)])
 
     with jax.named_scope("sum_a"):
         total = chunk(xpos, core) + ad[xpos].astype(F32)
+        one.wait_recv()
         for k in range(3):
-            one[k].wait_recv()
             total = total + a1[k].astype(F32)
         tiles = [total[r * 16 : (r + 1) * 16, k * 128 : (k + 1) * 128].astype(BF16) for r in range(3) for k in range(3)]
         for k in range(8):
             a2s[k, 0] = tiles[k]
             a2s[k, 1] = tiles[8]
-    three_ = [net.start(a2s.at[(z + k) % 8], a2.at[k - 1], zs(k)) for k in range(1, 8)]
+    three_ = net.many(a2, [(a2s.at[(z + k) % 8], a2.at[k - 1], zs(k)) for k in range(1, 8)])
 
     with jax.named_scope("sum_f"):
         lines = f0[lon].astype(F32)
+        two.wait_recv()
         for k in range(15):
-            two[k].wait_recv()
             lines = lines + f1[k].astype(F32)
         f3[z] = lines.astype(BF16)
-    five = [net.start(f3.at[z], f3.at[z], zs(k)) for k in range(1, 8)]
+    part = f3.at[pl.ds(0, 7)]
+    five = net.many(part, [(f3.at[z], f3.at[z], zs(k)) for k in range(1, 8)])
 
     with jax.named_scope("sum_z"):
         block = a2s[z].astype(F32)
+        three_.wait_recv()
         for k in range(7):
-            three_[k].wait_recv()
             block = block + a2[k].astype(F32)
         a3[z] = block[0].astype(BF16)
-    six = [net.start(a3.at[z], a3.at[z], zs(k)) for k in range(1, 8)]
+    six = net.many(a3.at[pl.ds(0, 7)], [(a3.at[z], a3.at[z], zs(k)) for k in range(1, 8)])
     a_out[xc, 8] = block[1].astype(BF16)
 
     with jax.named_scope("sum_p"):
         feat = p0[head].astype(F32)
+        pieces.wait_recv()
         for k in range(3):
-            pieces[k].wait_recv()
             feat = feat + p1[k].astype(F32)
         place_features(feat, v["lines"], own_out)
     net.settle()
     back = net.start(own_out.at[:, pl.ds(first, 6)], west_out, {"lon": (lon + step) % 16})
 
     with jax.named_scope("all_f"):
-        for k in range(7):
-            five[k].wait_recv()
-    part = f3.at[pl.ds(0, 7)]
+        five.wait_recv()
     mine = f_out.at[xc, pl.ds(0, 7)]
     arrive_f = [net.start(part, mine, at_grid(z, (xpos + k) % 4, core)) for k in range(1, 4)]
-    cross = [net.start(part, mine, partner)]
+    cross_f, cross_a = net.slot(), net.slot()
+    net.start(part, mine, partner, cross_f)
     f_out[xc] = f3[...]
     with jax.named_scope("all_a"):
-        for k in range(7):
-            six[k].wait_recv()
+        six.wait_recv()
     a_out[xc, 0:8] = a3[...]
     arrive = [net.start(a_out.at[xc], a_out.at[xc], at_grid(z, (xpos + k) % 4, core)) for k in range(1, 4)]
-    cross.append(net.start(a_out.at[xc], a_out.at[xc], partner))
+    net.start(a_out.at[xc], a_out.at[xc], partner, cross_a)
     with jax.named_scope("forward_x"):
-        for arrived, out, whole in ((arrive_f, f_out, False), (arrive, a_out, True)):
-            for k in range(1, 4):
-                there = ((xpos + 4 - k) % 4) * 2 + core
-                arrived[k - 1].wait_recv()
-                ref = out.at[there] if whole else out.at[there, pl.ds(0, 7)]
-                cross.append(net.start(ref, ref, partner))
+        for k in range(1, 4):
+            there = ((xpos + 4 - k) % 4) * 2 + core
+            arrive_f[k - 1].wait_recv()
+            ref = f_out.at[there, pl.ds(0, 7)]
+            net.start(ref, ref, partner, cross_f)
+        for k in range(1, 4):
+            there = ((xpos + 4 - k) % 4) * 2 + core
+            arrive[k - 1].wait_recv()
+            net.start(a_out.at[there], a_out.at[there], partner, cross_a)
+    cross = [net.group(cross_f, f_out.at[pl.ds(0, 4), pl.ds(0, 7)], partner), net.group(cross_a, a_out.at[pl.ds(0, 4)], partner)]
     net.settle()
     with jax.named_scope("last"):
         back.wait_recv()
@@ -501,7 +524,7 @@
             functools.partial(main_kernel, first),
             out_shape=(
                 jax.ShapeDtypeStruct((8, 9, 16, 128), BF16),
-                jax.ShapeDtypeStruct((8, 8, 16, 256), BF16),
+                jax.ShapeDtypeStruct((8, 8, 3, 8, 128), BF16),
                 jax.ShapeDtypeStruct((6, SLOTS, 8, 128), BF16),
                 jax.ShapeDtypeStruct((6, 6, 8, 128), BF16),
             ),

time: 52.9 us -> 50.4 us (0.953)
  Pallas kernels: 51.3 us -> 48.9 us
    pallas_call x1, Pallas kernels: 49 us -> 46.6 us  [per_device(): lax.cond(window_shift[0] <= 6, run(0), run(6), *args)]
where the time goes in v4:
time: 50.4 us
  Pallas kernels  48.9 us (97%)
  between operations  1.29 us (3%)
    pallas_call x1, Pallas kernels, per_device(): lax.cond(window_shift[0] <= 6, run(0), run(6), *args)  46.6 us
    pallas_call x1, Pallas kernels, finish(): pl.pallas_call(finish_kernel, out_shape=(jax.ShapeDtypeStruct((3, WIDTH,...  2.27 us

profile of v4, /device:TPU:1, one launch (start us, length us, event | category | flops | bytes accessed | tf_op | source)
XLA Modules:
  0.0 50.4 jit_solution(5398816846236004628)
XLA Ops:
  1.3 46.8 %conditional.1 = ((bf16[8,9,16,128]{3,2,1,0:T(8,128)(2,1)S(1)}, bf16[8,8,3,8,128]{4,3,2,1,0:T(8,128)(2,1)S(1)}, bf16[6,12,8,128]{3,2,1,0:T(8,128)(2,1)S(1)}, bf16[6,6,8,128]{3,2,1,0:T(8,128)(2,1)S(1)})) conditional(s32[]{:T(128)} %bitcast, (s32[1,4]{1,0:T(1,128)}, s32[1]{0:T(128)}, bf16[6,12,8,384]{3,2,1,0:T(8,128)(2,1)}, ...), branch_computations={%region_0.0_spmd, %region_1.0_spmd} | conditional | bytes 8 | solution.py:541
  1.5 46.6 %block_east.1 = (bf16[8,9,16,128]{3,2,1,0:T(8,128)(2,1)S(1)}, bf16[8,8,3,8,128]{4,3,2,1,0:T(8,128)(2,1)S(1)}, bf16[6,12,8,128]{3,2,1,0:T(8,128)(2,1)S(1)}, bf16[6,6,8,128]{3,2,1,0:T(8,128)(2,1)S(1)}) custom-call(s32[1,4]{1,0:T(1,128)} %get-tuple-element.35.types_ref, s32[1]{0:T(128)} %get-tuple-element.36.shift_ref, ...), custom_call_target="tpu_custom_call" | custom-call | tf_op jit(solution)/shard_map/cond/branch_1_fun/block_east/pallas_call | solution.py:541
  48.1 2.3 %finish.1 = (f32[3,96,384]{2,1,0:T(8,128)}, f32[96,384]{1,0:T(8,128)}, f32[3,64,3312]{2,1,0:T(8,128)}, bf16[6,12,8,96]{3,2,1,0:T(8,128)(2,1)}) custom-call(s32[1]{0:T(128)S(6)} %copy.19.shift_ref, bf16[8,9,16,128]{3,2,1,0:T(8,128)(2,1)S(1)} %get-tuple-element.54.sums, bf16[8,8,3,8,128]{4,3,2,1,0:T(8,128)(2,1)S(1)} %get-tuple-element.55.folded, ...), custom_call_target="tpu_custom_call" | custom-call | tf_op jit(solution)/shard_map/finish/pallas_call | solution.py:546

commit v5 on v4

--- a/solution.py
+++ b/solution.py
@@ -356,8 +356,8 @@
     a3=pltpu.VMEM((8, 16, 128), BF16),
     lines=pltpu.VMEM((576, 128), F32),
     f3=pltpu.VMEM((8, 3, 8, 128), BF16),
-    send=pltpu.SemaphoreType.DMA((21,)),
-    recv=pltpu.SemaphoreType.DMA((21,)),
+    send=pltpu.SemaphoreType.DMA((22,)),
+    recv=pltpu.SemaphoreType.DMA((22,)),
     load=pltpu.SemaphoreType.DMA((7,)),
     types=pltpu.SMEM((1, 4), jnp.int32),
     shift=pltpu.SMEM((1,), jnp.int32),
@@ -383,10 +383,11 @@
         pl.semaphore_wait(pltpu.get_barrier_semaphore(), met)
 
     giver = {"lon": (lon + 16 - step) % 16}
-    rows, cols = pl.ds((head // 2) * 3, 3), (head % 2) * 3
-    quarter = v["ge"].at[rows, pl.ds(cols, 3)]
-    halo = [net.start(v["gv"].at[rows, pl.ds(first + cols, 3)], quarter, giver)]
-    halo.append(net.start(v["xv"].at[:, pl.ds(first, 6)], v["xe"], giver))
+    reach, tail = pl.ds(first, 6), pl.ds(4, 2)
+    row = v["ge"].at[head]
+    halo = [net.start(v["gv"].at[head, reach], row, giver)]
+    halo.append(net.start(v["xv"].at[:, reach], v["xe"], giver))
+    halo.append(net.start(v["gv"].at[tail, reach], v["ge"].at[tail], giver))
     with jax.named_scope("bias"):
         for made in loads[2:5]:
             made.wait()
@@ -406,14 +407,14 @@
 
     with jax.named_scope("halo_q"):
         halo[0].wait_recv()
-    handed = [net.start(quarter, quarter, {"head": (head + j) % 4}) for j in range(1, 4)]
+    handed = [net.start(row, row, {"head": (head + j) % 4}) for j in range(1, 4)]
     with jax.named_scope("halo_x"):
         halo[1].wait_recv()
     with jax.named_scope("forward"):
         place_rows(v["xv"], v["xe"], shift, v["xs"], first, mixed)
         forward(v["xs"], wts, v["bias"], v["projs"], v["softs"], v["atts"])
     with jax.named_scope("halo_g"):
-        for made in handed:
+        for made in [halo[2], *handed]:
             made.wait_recv()
     with jax.named_scope("backward"):
         place_rows(v["gv"], v["ge"], shift, v["gs"], first, mixed)

time: 50.4 us -> 50.7 us (level)
  Pallas kernels: 48.9 us -> 49.5 us
    pallas_call x1, Pallas kernels: 46.6 us -> 47.2 us  [per_device(): lax.cond(window_shift[0] <= 6, run(0), run(6), *args)]
where the time goes in v5:
time: 50.7 us; the launch traced here: 51 us
  Pallas kernels  49.5 us (98%)
  between operations  1.29 us (3%)
    pallas_call x1, Pallas kernels, per_device(): lax.cond(window_shift[0] <= 6, run(0), run(6), *args)  47.2 us
    pallas_call x1, Pallas kernels, finish(): pl.pallas_call(finish_kernel, out_shape=(jax.ShapeDtypeStruct((3, WIDTH,...  2.27 us

profile of v5, /device:TPU:1, one launch (start us, length us, event | category | flops | bytes accessed | tf_op | source)
XLA Modules:
  0.0 51.0 jit_solution(12285267347211558905)
XLA Ops:
  1.3 47.4 %conditional.1 = ((bf16[8,9,16,128]{3,2,1,0:T(8,128)(2,1)S(1)}, bf16[8,8,3,8,128]{4,3,2,1,0:T(8,128)(2,1)S(1)}, bf16[6,12,8,128]{3,2,1,0:T(8,128)(2,1)S(1)}, bf16[6,6,8,128]{3,2,1,0:T(8,128)(2,1)S(1)})) conditional(s32[]{:T(128)} %bitcast, (s32[1,4]{1,0:T(1,128)}, s32[1]{0:T(128)}, bf16[6,12,8,384]{3,2,1,0:T(8,128)(2,1)}, ...), branch_computations={%region_0.0_spmd, %region_1.0_spmd} | conditional | bytes 8 | solution.py:542
  1.3 47.2 %block_west.1 = (bf16[8,9,16,128]{3,2,1,0:T(8,128)(2,1)S(1)}, bf16[8,8,3,8,128]{4,3,2,1,0:T(8,128)(2,1)S(1)}, bf16[6,12,8,128]{3,2,1,0:T(8,128)(2,1)S(1)}, bf16[6,6,8,128]{3,2,1,0:T(8,128)(2,1)S(1)}) custom-call(s32[1,4]{1,0:T(1,128)} %get-tuple-element.28.types_ref, s32[1]{0:T(128)} %get-tuple-element.29.shift_ref, ...), custom_call_target="tpu_custom_call" | custom-call | tf_op jit(solution)/shard_map/cond/branch_0_fun/block_west/pallas_call | solution.py:542
  48.7 2.3 %finish.1 = (f32[3,96,384]{2,1,0:T(8,128)}, f32[96,384]{1,0:T(8,128)}, f32[3,64,3312]{2,1,0:T(8,128)}, bf16[6,12,8,96]{3,2,1,0:T(8,128)(2,1)}) custom-call(s32[1]{0:T(128)S(6)} %copy.19.shift_ref, bf16[8,9,16,128]{3,2,1,0:T(8,128)(2,1)S(1)} %get-tuple-element.54.sums, bf16[8,8,3,8,128]{4,3,2,1,0:T(8,128)(2,1)S(1)} %get-tuple-element.55.folded, ...), custom_call_target="tpu_custom_call" | custom-call | tf_op jit(solution)/shard_map/finish/pallas_call | solution.py:547

commit v6 on v4

--- a/solution.py
+++ b/solution.py
@@ -313,9 +313,10 @@
 def reduce_peers():
     lon, lat, head, z, high, x, core = place()
     xc = x * 2 + core
-    peers = [{"lon": (lon + k) % 16} for k in range(1, 16)]
+    peers = [{"lon": (lon + k) % 16} for k in (1, 15)]
+    peers += [{"head": (head + k) % 4} for k in range(1, 4)]
+    peers += [{"lon": (lon + k) % 16} for k in (8, 7, 9, 6, 10, 5, 11, 4, 12, 3, 13, 2, 14)]
     peers += [at_grid(z, ((xc + k) % 8) // 2, (xc + k) % 2) for k in range(1, 8)]
-    peers += [{"head": (head + k) % 4} for k in range(1, 4)]
     return peers
 
 
@@ -370,13 +371,15 @@
     xc = xpos * 2 + core
     step = 1 if first == 0 else 15
     net = Links(v["send"], v["recv"])
-    met = greet(reduce_peers())
     loads = []
     given = ((g, "gv"), (x, "xv"), (types_ref, "types"), (shift_ref, "shift"), (table, "tabv"), (wt, "wtv"), (wo, "wov"))
     for src, dst in given:
-        made = pltpu.make_async_copy(src, v[dst], v["load"].at[len(loads)])
+        loads.append(pltpu.make_async_copy(src, v[dst], v["load"].at[len(loads)]))
+    loads[0].start()
+    loads[1].start()
+    met = greet(reduce_peers())
+    for made in loads[2:]:
         made.start()
-        loads.append(made)
     with jax.named_scope("enter"):
         for made in loads[0:2]:
             made.wait()
@@ -506,11 +509,11 @@
             arrive[k - 1].wait_recv()
             net.start(a_out.at[there], a_out.at[there], partner, cross_a)
     cross = [net.group(cross_f, f_out.at[pl.ds(0, 4), pl.ds(0, 7)], partner), net.group(cross_a, a_out.at[pl.ds(0, 4)], partner)]
-    net.settle()
     with jax.named_scope("last"):
         back.wait_recv()
         for made in cross:
             made.wait_recv()
+    net.settle()
 
 
 def per_device(features, attend_weight, output_weight, bias_table, bias_type, window_shift, grad_out):

time: 50.4 us -> 50.5 us (level)
  no operation moved by 1% of the time
where the time goes in v6:
time: 50.5 us; the launch traced here: 50.3 us
  Pallas kernels  48.9 us (97%)
  between operations  1.29 us (3%)
    pallas_call x1, Pallas kernels, per_device(): lax.cond(window_shift[0] <= 6, run(0), run(6), *args)  46.6 us
    pallas_call x1, Pallas kernels, finish(): pl.pallas_call(finish_kernel, out_shape=(jax.ShapeDtypeStruct((3, WIDTH,...  2.26 us

profile of v6, /device:TPU:1, one launch (start us, length us, event | category | flops | bytes accessed | tf_op | source)
XLA Modules:
  0.0 50.3 jit_solution(16199812457615011867)
XLA Ops:
  1.3 46.8 %conditional.1 = ((bf16[8,9,16,128]{3,2,1,0:T(8,128)(2,1)S(1)}, bf16[8,8,3,8,128]{4,3,2,1,0:T(8,128)(2,1)S(1)}, bf16[6,12,8,128]{3,2,1,0:T(8,128)(2,1)S(1)}, bf16[6,6,8,128]{3,2,1,0:T(8,128)(2,1)S(1)})) conditional(s32[]{:T(128)} %bitcast, (s32[1,4]{1,0:T(1,128)}, s32[1]{0:T(128)}, bf16[6,12,8,384]{3,2,1,0:T(8,128)(2,1)}, ...), branch_computations={%region_0.0_spmd, %region_1.0_spmd} | conditional | bytes 8 | solution.py:544
  1.5 46.6 %block_east.1 = (bf16[8,9,16,128]{3,2,1,0:T(8,128)(2,1)S(1)}, bf16[8,8,3,8,128]{4,3,2,1,0:T(8,128)(2,1)S(1)}, bf16[6,12,8,128]{3,2,1,0:T(8,128)(2,1)S(1)}, bf16[6,6,8,128]{3,2,1,0:T(8,128)(2,1)S(1)}) custom-call(s32[1,4]{1,0:T(1,128)} %get-tuple-element.35.types_ref, s32[1]{0:T(128)} %get-tuple-element.36.shift_ref, ...), custom_call_target="tpu_custom_call" | custom-call | tf_op jit(solution)/shard_map/cond/branch_1_fun/block_east/pallas_call | solution.py:544
  48.1 2.3 %finish.1 = (f32[3,96,384]{2,1,0:T(8,128)}, f32[96,384]{1,0:T(8,128)}, f32[3,64,3312]{2,1,0:T(8,128)}, bf16[6,12,8,96]{3,2,1,0:T(8,128)(2,1)}) custom-call(s32[1]{0:T(128)S(6)} %copy.19.shift_ref, bf16[8,9,16,128]{3,2,1,0:T(8,128)(2,1)S(1)} %get-tuple-element.54.sums, bf16[8,8,3,8,128]{4,3,2,1,0:T(8,128)(2,1)S(1)} %get-tuple-element.55.folded, ...), custom_call_target="tpu_custom_call" | custom-call | tf_op jit(solution)/shard_map/finish/pallas_call | solution.py:549

commit v7 on v4

--- a/solution.py
+++ b/solution.py
@@ -386,7 +386,9 @@
     rows, cols = pl.ds((head // 2) * 3, 3), (head % 2) * 3
     quarter = v["ge"].at[rows, pl.ds(cols, 3)]
     halo = [net.start(v["gv"].at[rows, pl.ds(first + cols, 3)], quarter, giver)]
-    halo.append(net.start(v["xv"].at[:, pl.ds(first, 6)], v["xe"], giver))
+    skip = 0 if first == 0 else 1
+    near, spot = pl.ds(first + skip, 6 - skip), pl.ds(skip, 6 - skip)
+    halo.append(net.start(v["xv"].at[:, near], v["xe"].at[:, spot], giver))
     with jax.named_scope("bias"):
         for made in loads[2:5]:
             made.wait()
@@ -395,7 +397,7 @@
         expand_bias(types, shift, v["tabv"], v["tabw"], v["spread"], v["maps"], v["bias"])
     mixed = [c for c in range(first, first + 6)]
     still = [c for c in range(SLOTS) if c not in mixed]
-    place_rows(v["xv"], None, shift, v["xs"], first, still)
+    place_rows(v["xv"], None, shift, v["xs"], first, still + mixed[:skip])
     place_rows(v["gv"], None, shift, v["gs"], first, still)
     with jax.named_scope("still"):
         loads[5].wait()
@@ -410,7 +412,7 @@
     with jax.named_scope("halo_x"):
         halo[1].wait_recv()
     with jax.named_scope("forward"):
-        place_rows(v["xv"], v["xe"], shift, v["xs"], first, mixed)
+        place_rows(v["xv"], v["xe"], shift, v["xs"], first, mixed[skip:])
         forward(v["xs"], wts, v["bias"], v["projs"], v["softs"], v["atts"])
     with jax.named_scope("halo_g"):
         for made in handed:
@@ -481,7 +483,7 @@
             feat = feat + p1[k].astype(F32)
         place_features(feat, v["lines"], own_out)
     net.settle()
-    back = net.start(own_out.at[:, pl.ds(first, 6)], west_out, {"lon": (lon + step) % 16})
+    back = net.start(own_out.at[:, near], west_out.at[:, spot], {"lon": (lon + step) % 16})
 
     with jax.named_scope("all_f"):
         five.wait_recv()

time: 50.4 us -> 50.5 us (level)
  no operation moved by 1% of the time
where the time goes in v7:
time: 50.5 us; the launch traced here: 50.4 us
  Pallas kernels  48.9 us (97%)
  between operations  1.29 us (3%)
    pallas_call x1, Pallas kernels, per_device(): lax.cond(window_shift[0] <= 6, run(0), run(6), *args)  46.6 us
    pallas_call x1, Pallas kernels, finish(): pl.pallas_call(finish_kernel, out_shape=(jax.ShapeDtypeStruct((3, WIDTH,...  2.27 us

profile of v7, /device:TPU:1, one launch (start us, length us, event | category | flops | bytes accessed | tf_op | source)
XLA Modules:
  0.0 50.4 jit_solution(3566812489214117694)
XLA Ops:
  1.3 46.8 %conditional.1 = ((bf16[8,9,16,128]{3,2,1,0:T(8,128)(2,1)S(1)}, bf16[8,8,3,8,128]{4,3,2,1,0:T(8,128)(2,1)S(1)}, bf16[6,12,8,128]{3,2,1,0:T(8,128)(2,1)S(1)}, bf16[6,6,8,128]{3,2,1,0:T(8,128)(2,1)S(1)})) conditional(s32[]{:T(128)} %bitcast, (s32[1,4]{1,0:T(1,128)}, s32[1]{0:T(128)}, bf16[6,12,8,384]{3,2,1,0:T(8,128)(2,1)}, ...), branch_computations={%region_0.0_spmd, %region_1.0_spmd} | conditional | bytes 8 | solution.py:543
  1.5 46.6 %block_east.1 = (bf16[8,9,16,128]{3,2,1,0:T(8,128)(2,1)S(1)}, bf16[8,8,3,8,128]{4,3,2,1,0:T(8,128)(2,1)S(1)}, bf16[6,12,8,128]{3,2,1,0:T(8,128)(2,1)S(1)}, bf16[6,6,8,128]{3,2,1,0:T(8,128)(2,1)S(1)}) custom-call(s32[1,4]{1,0:T(1,128)} %get-tuple-element.35.types_ref, s32[1]{0:T(128)} %get-tuple-element.36.shift_ref, ...), custom_call_target="tpu_custom_call" | custom-call | tf_op jit(solution)/shard_map/cond/branch_1_fun/block_east/pallas_call | solution.py:543
  48.1 2.3 %finish.1 = (f32[3,96,384]{2,1,0:T(8,128)}, f32[96,384]{1,0:T(8,128)}, f32[3,64,3312]{2,1,0:T(8,128)}, bf16[6,12,8,96]{3,2,1,0:T(8,128)(2,1)}) custom-call(s32[1]{0:T(128)S(6)} %copy.19.shift_ref, bf16[8,9,16,128]{3,2,1,0:T(8,128)(2,1)S(1)} %get-tuple-element.54.sums, bf16[8,8,3,8,128]{4,3,2,1,0:T(8,128)(2,1)S(1)} %get-tuple-element.55.folded, ...), custom_call_target="tpu_custom_call" | custom-call | tf_op jit(solution)/shard_map/finish/pallas_call | solution.py:548

commit v8 on v7

--- a/solution.py
+++ b/solution.py
@@ -482,7 +482,6 @@
         for k in range(3):
             feat = feat + p1[k].astype(F32)
         place_features(feat, v["lines"], own_out)
-    net.settle()
     back = net.start(own_out.at[:, near], west_out.at[:, spot], {"lon": (lon + step) % 16})
 
     with jax.named_scope("all_f"):

time: 50.5 us -> 50.4 us (level)
  no operation moved by 1% of the time
where the time goes in v8:
time: 50.4 us
  Pallas kernels  48.9 us (97%)
  between operations  1.29 us (3%)
    pallas_call x1, Pallas kernels, per_device(): lax.cond(window_shift[0] <= 6, run(0), run(6), *args)  46.7 us
    pallas_call x1, Pallas kernels, finish(): pl.pallas_call(finish_kernel, out_shape=(jax.ShapeDtypeStruct((3, WIDTH,...  2.27 us

profile of v8, /device:TPU:1, one launch (start us, length us, event | category | flops | bytes accessed | tf_op | source)
XLA Modules:
  0.0 50.4 jit_solution(2042907910480224717)
XLA Ops:
  1.3 46.9 %conditional.1 = ((bf16[8,9,16,128]{3,2,1,0:T(8,128)(2,1)S(1)}, bf16[8,8,3,8,128]{4,3,2,1,0:T(8,128)(2,1)S(1)}, bf16[6,12,8,128]{3,2,1,0:T(8,128)(2,1)S(1)}, bf16[6,6,8,128]{3,2,1,0:T(8,128)(2,1)S(1)})) conditional(s32[]{:T(128)} %bitcast, (s32[1,4]{1,0:T(1,128)}, s32[1]{0:T(128)}, bf16[6,12,8,384]{3,2,1,0:T(8,128)(2,1)}, ...), branch_computations={%region_0.0_spmd, %region_1.0_spmd} | conditional | bytes 8 | solution.py:542
  1.5 46.7 %block_east.1 = (bf16[8,9,16,128]{3,2,1,0:T(8,128)(2,1)S(1)}, bf16[8,8,3,8,128]{4,3,2,1,0:T(8,128)(2,1)S(1)}, bf16[6,12,8,128]{3,2,1,0:T(8,128)(2,1)S(1)}, bf16[6,6,8,128]{3,2,1,0:T(8,128)(2,1)S(1)}) custom-call(s32[1,4]{1,0:T(1,128)} %get-tuple-element.35.types_ref, s32[1]{0:T(128)} %get-tuple-element.36.shift_ref, ...), custom_call_target="tpu_custom_call" | custom-call | tf_op jit(solution)/shard_map/cond/branch_1_fun/block_east/pallas_call | solution.py:542
  48.1 2.3 %finish.1 = (f32[3,96,384]{2,1,0:T(8,128)}, f32[96,384]{1,0:T(8,128)}, f32[3,64,3312]{2,1,0:T(8,128)}, bf16[6,12,8,96]{3,2,1,0:T(8,128)(2,1)}) custom-call(s32[1]{0:T(128)S(6)} %copy.19.shift_ref, bf16[8,9,16,128]{3,2,1,0:T(8,128)(2,1)S(1)} %get-tuple-element.54.sums, bf16[8,8,3,8,128]{4,3,2,1,0:T(8,128)(2,1)S(1)} %get-tuple-element.55.folded, ...), custom_call_target="tpu_custom_call" | custom-call | tf_op jit(solution)/shard_map/finish/pallas_call | solution.py:547
